TPU v7x, 128 devices: a whole 4x4x4 slice. The times are simulated.
128 devices in a mesh: tm: 16 (over y, z), port: 8 (over x, core).
Axes of the slice: x: 4, y: 4, z: 4, core: 2. Of those that a mesh axis runs over, the one named last changes fastest.
Arguments:
- voltages: float32 [256, 262144], P('port', 'tm'), may hold values from -6 to 6
- currents: float32 [256, 262144], P('port', 'tm'), may hold values from -0.12 to 0.12
- impedance: float32 [256], P('port'), may hold values from 25 to 100
- freq_index: int32 [2048], replicated, may hold values from 1 to 131071
- window_start: int32 [256], P('port'), may hold values from 0 to 131071
- pairing: int32 [256], P('port'), may hold values from 0 to 255
Outputs:
- scattering: float32 [2, 256, 2048], P(None, 'port', 'tm')
All inputs are finite; a program needn't handle non-finite values.
Results may differ from a plain program's by a relative error of at most 0.011.
Values sent between devices are 32-bit elements; how exact they have to be, the bound alone decides.
No kernel may reach another device: no remote copies, remote signals or barrier semaphores. Data moves between devices by JAX's collectives and lax.ppermute only.
A program may use at most 128 MiB of HBM per device.

v0:
```python
import math

import jax
import jax.numpy as jnp
from jax import lax
from jax.sharding import PartitionSpec as P


def in_blocks(shard, dim, size):
    before, after = (shard.shape[:dim], shard.shape[dim + 1 :])
    return jnp.moveaxis(shard.reshape(*before, size, -1, *after), dim, 0)


def summed_on_arrival(shard, axis, dim):
    size = lax.axis_size(axis)
    parts = lax.all_to_all(in_blocks(shard, dim, size), axis, 0, 0, tiled=True)
    return jnp.sum(parts, axis=0)


def sent_together(arrays, axis, dim, along):
    ends, at = ([], 0)
    for a in arrays[:-1]:
        at += a.shape[along]
        ends.append(at)
    both = jnp.concatenate(arrays, axis=along)
    return tuple(jnp.split(summed_on_arrival(both, axis, dim), ends, axis=along))


def from_everyone(shard, axis):
    copies = jnp.broadcast_to(shard, (lax.axis_size(axis), *shard.shape))
    return lax.all_to_all(copies, axis, split_axis=0, concat_axis=0, tiled=True)


def of_everyone(shard, axis):
    everything = from_everyone(shard, axis)
    return jnp.sum(everything, axis=0)


def side_by_side(arrays, axis, dim, along):
    widths = [math.prod(a.shape[along:]) for a in arrays]
    both = jnp.concatenate(
        [a.reshape(*a.shape[:along], w) for a, w in zip(arrays, widths)], axis=along
    )
    result = lax.all_gather(both, axis, axis=dim, tiled=True)
    parts = jnp.split(result, [sum(widths[:k]) for k in range(1, len(widths))], axis=along)
    return tuple(
        (b.reshape(*result.shape[:along], *a.shape[along:]) for a, b in zip(arrays, parts))
    )


def angles(freq_index, times, total):
    high = freq_index // 512
    low = freq_index % 512
    stride = times * 512 % total
    phase = (stride[:, None] * high[None, :] % total + times[:, None] * low[None, :]) % total
    angle = phase.astype(jnp.float32) * (2.0 * math.pi / total)
    return (jnp.cos(angle), jnp.sin(angle))


def waves(v_re, v_im, c_re, c_im, impedance):
    zcol = impedance[:, None]
    root = 2.0 * jnp.sqrt(zcol)
    a_re = (v_re + zcol * c_re) / root
    a_im = (v_im + zcol * c_im) / root
    b_re = (v_re - zcol * c_re) / root
    b_im = (v_im - zcol * c_im) / root
    return (a_re, a_im, b_re, b_im)


def body(voltages, currents, impedance, freq_index, window_start, pairing):
    local_ports, local_times = voltages.shape
    width = freq_index.shape[0]
    tm_count = lax.axis_size("tm")
    total = local_times * tm_count
    first = lax.axis_index("tm") * local_times
    local = first + jnp.arange(local_times, dtype=jnp.int32)
    gate = local[None, :] >= window_start[:, None]
    gated_v = jnp.where(gate, voltages, 0.0).astype(jnp.bfloat16)
    gated_c = jnp.where(gate, currents, 0.0).astype(jnp.bfloat16)
    block = math.gcd(local_times, 4096)
    inner = min(block, 128)
    groups = block // inner
    base_cos, base_sin = angles(freq_index, jnp.arange(inner, dtype=jnp.int32), total)

    def accumulate(index, carry):
        start = index * block
        offsets = first + start + inner * jnp.arange(groups, dtype=jnp.int32)
        turn_cos, turn_sin = angles(freq_index, offsets, total)
        cos_part = (
            turn_cos[:, None, :] * base_cos[None] - turn_sin[:, None, :] * base_sin[None]
        ).astype(jnp.bfloat16)
        sin_part = (
            -(turn_sin[:, None, :] * base_cos[None] + turn_cos[:, None, :] * base_sin[None])
        ).astype(jnp.bfloat16)
        table = jnp.concatenate([cos_part, sin_part], axis=2).reshape(block, 2 * width)
        part_v = lax.dynamic_slice_in_dim(gated_v, start, block, 1)
        part_c = lax.dynamic_slice_in_dim(gated_c, start, block, 1)
        return (
            carry[0] + jnp.dot(part_v, table, preferred_element_type=jnp.float32),
            carry[1] + jnp.dot(part_c, table, preferred_element_type=jnp.float32),
        )

    empty = jnp.zeros((local_ports, 2 * width), jnp.float32)
    sum_v, sum_c = lax.fori_loop(0, local_times // block, accumulate, (empty, empty))
    scale = 1.0 / math.sqrt(total)
    split_v = sum_v.reshape(local_ports, 2, width)
    split_c = sum_c.reshape(local_ports, 2, width)
    share_v, share_c = sent_together((split_v, split_c), "tm", 2, 0)
    share_v = share_v * scale
    share_c = share_c * scale
    a_re, a_im, b_re, b_im = waves(
        share_v[:, 0], share_v[:, 1], share_c[:, 0], share_c[:, 1], impedance
    )
    power = a_re * a_re + a_im * a_im
    summed = of_everyone(jnp.sum(power, axis=1), "tm")
    mean_power = summed / width + 1e-06
    every_re, every_im, every_mean = side_by_side((a_re, a_im, mean_power), "port", 0, 1)
    q_re = jnp.take(every_re, pairing, axis=0)
    q_im = jnp.take(every_im, pairing, axis=0)
    q_mean = jnp.take(every_mean, pairing, axis=0)
    q_power = q_re * q_re + q_im * q_im
    denom = jnp.maximum(q_power, 0.1 * q_mean[:, None])
    s_re = (b_re * q_re + b_im * q_im) / denom
    s_im = (b_im * q_re - b_re * q_im) / denom
    return jnp.stack([s_re, s_im], axis=0)


def solution(mesh):
    placed = (P("port", "tm"), P("port", "tm"), P("port"), P(), P("port"), P("port"))
    return jax.shard_map(
        body, mesh=mesh, in_specs=placed, out_specs=P(None, "port", "tm"), check_vma=False
    )
```

profile of v0, /device:TPU:0, one launch (start us, length us, event | category | flops | bytes accessed | tf_op | source)
XLA Modules:
  0.0 249.0 jit_solution(18248575543977199948)
XLA Ops:
  0.0 0.7 add_select_fusion.6
  0.7 2.6 %fusion.32 = (bf16[32,16384]{1,0:T(8,128)(2,1)S(1)}, bf16[32,16384]{1,0:T(8,128)(2,1)S(1)}) fusion(f32[32,16384]{1,0:T(8,128)} %param.11, s32[16384]{0:T(1024)S(1)} %iota_add_fusion, s32[32]{0:T(128)} %param.14, f32[32,16384]{1,0:T(8,128)} %param.10), kind=kLoop, calls=%fused_computation.65 | loop fusion | flops 1572864 | bytes 6357120 | tf_op jit(solution)/shard_map/convert_element_type | solution.py:79
  3.4 0.0 copy-start
  3.4 0.0 copy-start.1
  3.4 189.6 %while.22 = (s32[]{:T(128)}, f32[32,4096]{1,0:T(8,128)S(1)}, f32[32,4096]{1,0:T(8,128)S(1)}, bf16[32,16384]{1,0:T(8,128)(2,1)S(1)}, s32[]{:T(128)}, /*index=5*/s...) while((s32[]{:T(128)}, f32[32,4096]{1,0:T(8,128)S(1)}, ...), condition=%wide.region_1.2_spmd.clone.clone.clone, body=%wide.region_0.1_spmd.clone.clone.clone.sunk | while | flops 2366616064 | bytes 108614880 | solution.py:104
  3.4 0.7 add_select_fusion.9
  4.2 1.2 fusion.48
  5.4 4.6 %fusion.47 = (f32[128,2048]{1,0:T(8,128)S(1)}, f32[128,2048]{1,0:T(8,128)S(1)}) fusion(s32[2048]{0:T(1024)S(1)} %get-tuple-element.662, s32[2048]{0:T(1024)S(1)} %get-tuple-element.660, s32[128]{0:T(128)S(1)} %get-tuple-element.661), kind=kLoop, calls=%fused_computation.26.clone.1 | loop fusion | flops 7077888 | bytes 2114048 | tf_op jit(solution)/shard_map/cos | solution.py:57
  10.0 15.4 %subtract_convert_fusion.2 = (bf16[32,128,2048]{2,1,0:T(8,128)(2,1)}, bf16[32,128,2048]{2,1,0:T(8,128)(2,1)}) fusion(f32[128,2048]{1,0:T(8,128)S(1)} %get-tuple-element.606, f32[32,2048]{1,0:T(8,128)S(1)} %get-tuple-element.611, f32[128,2048]{1,0:T(8,128)S(1)} %get-tuple-element.612, f32[32,2048]{1,0:T(8,128)S(1)} %get-tuple-element.613), kind=kLoop, calls=%fused_computation.7.clone.1 | loop fusion | flops 75497472 | bytes 36175872 | tf_op jit(solution)/shard_map/while/body/eval_jaxpr/convert_element_type | solution.py:91
  25.4 12.7 %fusion.50 = f32[32,4096]{1,0:T(8,128)S(1)} fusion(bf16[4096,2048]{1,0:T(8,128)(2,1)} %bitcast.76, bf16[4096,2048]{1,0:T(8,128)(2,1)} %bitcast.74, f32[32,4096]{1,0:T(8,128)S(1)} %get-tuple-element.635, bf16[32,16384]{1,0:T(8,128)(2,1)S(1)} %get-tuple-element.659, s32[]{:T(128)S(6)} %select_n.544, pred[]{:T(512)S(6)} %compare.43), kind=kOutput, calls=%fused_computation.11.clone.1 | convolution fusion | flops 1141112832 | bytes 34865156 | tf_op jit(solution)/shard_map/while/body/eval_jaxpr/dot_general | solution.py:100
  38.1 12.7 %fusion.49 = f32[32,4096]{1,0:T(8,128)S(1)} fusion(bf16[4096,2048]{1,0:T(8,128)(2,1)} %bitcast.77, bf16[4096,2048]{1,0:T(8,128)(2,1)} %bitcast.75, f32[32,4096]{1,0:T(8,128)S(1)} %get-tuple-element.634, bf16[32,16384]{1,0:T(8,128)(2,1)S(1)} %get-tuple-element.653, s32[]{:T(128)S(6)} %select_n.544, pred[]{:T(512)S(6)} %compare.43), kind=kOutput, calls=%fused_computation.10.clone.1 | convolution fusion | flops 1141112832 | bytes 34865156 | tf_op jit(solution)/shard_map/while/body/eval_jaxpr/dot_general | solution.py:99
  50.9 0.7 add_select_fusion.9
  51.6 1.2 fusion.48
  52.8 4.6 %fusion.47 = (f32[128,2048]{1,0:T(8,128)S(1)}, f32[128,2048]{1,0:T(8,128)S(1)}) fusion(s32[2048]{0:T(1024)S(1)} %get-tuple-element.662, s32[2048]{0:T(1024)S(1)} %get-tuple-element.660, s32[128]{0:T(128)S(1)} %get-tuple-element.661), kind=kLoop, calls=%fused_computation.26.clone.1 | loop fusion | flops 7077888 | bytes 2114048 | tf_op jit(solution)/shard_map/cos | solution.py:57
  57.4 15.4 %subtract_convert_fusion.2 = (bf16[32,128,2048]{2,1,0:T(8,128)(2,1)}, bf16[32,128,2048]{2,1,0:T(8,128)(2,1)}) fusion(f32[128,2048]{1,0:T(8,128)S(1)} %get-tuple-element.606, f32[32,2048]{1,0:T(8,128)S(1)} %get-tuple-element.611, f32[128,2048]{1,0:T(8,128)S(1)} %get-tuple-element.612, f32[32,2048]{1,0:T(8,128)S(1)} %get-tuple-element.613), kind=kLoop, calls=%fused_computation.7.clone.1 | loop fusion | flops 75497472 | bytes 36175872 | tf_op jit(solution)/shard_map/while/body/eval_jaxpr/convert_element_type | solution.py:91
  72.8 12.7 %fusion.50 = f32[32,4096]{1,0:T(8,128)S(1)} fusion(bf16[4096,2048]{1,0:T(8,128)(2,1)} %bitcast.76, bf16[4096,2048]{1,0:T(8,128)(2,1)} %bitcast.74, f32[32,4096]{1,0:T(8,128)S(1)} %get-tuple-element.635, bf16[32,16384]{1,0:T(8,128)(2,1)S(1)} %get-tuple-element.659, s32[]{:T(128)S(6)} %select_n.544, pred[]{:T(512)S(6)} %compare.43), kind=kOutput, calls=%fused_computation.11.clone.1 | convolution fusion | flops 1141112832 | bytes 34865156 | tf_op jit(solution)/shard_map/while/body/eval_jaxpr/dot_general | solution.py:100
  85.5 12.7 %fusion.49 = f32[32,4096]{1,0:T(8,128)S(1)} fusion(bf16[4096,2048]{1,0:T(8,128)(2,1)} %bitcast.77, bf16[4096,2048]{1,0:T(8,128)(2,1)} %bitcast.75, f32[32,4096]{1,0:T(8,128)S(1)} %get-tuple-element.634, bf16[32,16384]{1,0:T(8,128)(2,1)S(1)} %get-tuple-element.653, s32[]{:T(128)S(6)} %select_n.544, pred[]{:T(512)S(6)} %compare.43), kind=kOutput, calls=%fused_computation.10.clone.1 | convolution fusion | flops 1141112832 | bytes 34865156 | tf_op jit(solution)/shard_map/while/body/eval_jaxpr/dot_general | solution.py:99
  98.3 0.7 add_select_fusion.9
  99.0 1.2 fusion.48
  100.2 4.6 %fusion.47 = (f32[128,2048]{1,0:T(8,128)S(1)}, f32[128,2048]{1,0:T(8,128)S(1)}) fusion(s32[2048]{0:T(1024)S(1)} %get-tuple-element.662, s32[2048]{0:T(1024)S(1)} %get-tuple-element.660, s32[128]{0:T(128)S(1)} %get-tuple-element.661), kind=kLoop, calls=%fused_computation.26.clone.1 | loop fusion | flops 7077888 | bytes 2114048 | tf_op jit(solution)/shard_map/cos | solution.py:57
  104.8 15.4 %subtract_convert_fusion.2 = (bf16[32,128,2048]{2,1,0:T(8,128)(2,1)}, bf16[32,128,2048]{2,1,0:T(8,128)(2,1)}) fusion(f32[128,2048]{1,0:T(8,128)S(1)} %get-tuple-element.606, f32[32,2048]{1,0:T(8,128)S(1)} %get-tuple-element.611, f32[128,2048]{1,0:T(8,128)S(1)} %get-tuple-element.612, f32[32,2048]{1,0:T(8,128)S(1)} %get-tuple-element.613), kind=kLoop, calls=%fused_computation.7.clone.1 | loop fusion | flops 75497472 | bytes 36175872 | tf_op jit(solution)/shard_map/while/body/eval_jaxpr/convert_element_type | solution.py:91
  120.2 12.7 %fusion.50 = f32[32,4096]{1,0:T(8,128)S(1)} fusion(bf16[4096,2048]{1,0:T(8,128)(2,1)} %bitcast.76, bf16[4096,2048]{1,0:T(8,128)(2,1)} %bitcast.74, f32[32,4096]{1,0:T(8,128)S(1)} %get-tuple-element.635, bf16[32,16384]{1,0:T(8,128)(2,1)S(1)} %get-tuple-element.659, s32[]{:T(128)S(6)} %select_n.544, pred[]{:T(512)S(6)} %compare.43), kind=kOutput, calls=%fused_computation.11.clone.1 | convolution fusion | flops 1141112832 | bytes 34865156 | tf_op jit(solution)/shard_map/while/body/eval_jaxpr/dot_general | solution.py:100
  132.9 12.7 %fusion.49 = f32[32,4096]{1,0:T(8,128)S(1)} fusion(bf16[4096,2048]{1,0:T(8,128)(2,1)} %bitcast.77, bf16[4096,2048]{1,0:T(8,128)(2,1)} %bitcast.75, f32[32,4096]{1,0:T(8,128)S(1)} %get-tuple-element.634, bf16[32,16384]{1,0:T(8,128)(2,1)S(1)} %get-tuple-element.653, s32[]{:T(128)S(6)} %select_n.544, pred[]{:T(512)S(6)} %compare.43), kind=kOutput, calls=%fused_computation.10.clone.1 | convolution fusion | flops 1141112832 | bytes 34865156 | tf_op jit(solution)/shard_map/while/body/eval_jaxpr/dot_general | solution.py:99
  145.7 0.7 add_select_fusion.9
  146.4 1.2 fusion.48
  147.6 4.6 %fusion.47 = (f32[128,2048]{1,0:T(8,128)S(1)}, f32[128,2048]{1,0:T(8,128)S(1)}) fusion(s32[2048]{0:T(1024)S(1)} %get-tuple-element.662, s32[2048]{0:T(1024)S(1)} %get-tuple-element.660, s32[128]{0:T(128)S(1)} %get-tuple-element.661), kind=kLoop, calls=%fused_computation.26.clone.1 | loop fusion | flops 7077888 | bytes 2114048 | tf_op jit(solution)/shard_map/cos | solution.py:57
  152.2 15.4 %subtract_convert_fusion.2 = (bf16[32,128,2048]{2,1,0:T(8,128)(2,1)}, bf16[32,128,2048]{2,1,0:T(8,128)(2,1)}) fusion(f32[128,2048]{1,0:T(8,128)S(1)} %get-tuple-element.606, f32[32,2048]{1,0:T(8,128)S(1)} %get-tuple-element.611, f32[128,2048]{1,0:T(8,128)S(1)} %get-tuple-element.612, f32[32,2048]{1,0:T(8,128)S(1)} %get-tuple-element.613), kind=kLoop, calls=%fused_computation.7.clone.1 | loop fusion | flops 75497472 | bytes 36175872 | tf_op jit(solution)/shard_map/while/body/eval_jaxpr/convert_element_type | solution.py:91
  167.6 12.7 %fusion.50 = f32[32,4096]{1,0:T(8,128)S(1)} fusion(bf16[4096,2048]{1,0:T(8,128)(2,1)} %bitcast.76, bf16[4096,2048]{1,0:T(8,128)(2,1)} %bitcast.74, f32[32,4096]{1,0:T(8,128)S(1)} %get-tuple-element.635, bf16[32,16384]{1,0:T(8,128)(2,1)S(1)} %get-tuple-element.659, s32[]{:T(128)S(6)} %select_n.544, pred[]{:T(512)S(6)} %compare.43), kind=kOutput, calls=%fused_computation.11.clone.1 | convolution fusion | flops 1141112832 | bytes 34865156 | tf_op jit(solution)/shard_map/while/body/eval_jaxpr/dot_general | solution.py:100
  180.3 12.7 %fusion.49 = f32[32,4096]{1,0:T(8,128)S(1)} fusion(bf16[4096,2048]{1,0:T(8,128)(2,1)} %bitcast.77, bf16[4096,2048]{1,0:T(8,128)(2,1)} %bitcast.75, f32[32,4096]{1,0:T(8,128)S(1)} %get-tuple-element.634, bf16[32,16384]{1,0:T(8,128)(2,1)S(1)} %get-tuple-element.653, s32[]{:T(128)S(6)} %select_n.544, pred[]{:T(512)S(6)} %compare.43), kind=kOutput, calls=%fused_computation.10.clone.1 | convolution fusion | flops 1141112832 | bytes 34865156 | tf_op jit(solution)/shard_map/while/body/eval_jaxpr/dot_general | solution.py:99
  193.0 0.1 copy.32
  193.1 0.1 copy.33
  193.2 0.1 maximum_bitcast_fusion
  193.3 1.5 copy.23
  194.8 8.2 %all-to-all-start = ((f32[16,64,2,128]{3,2,1,0:T(2,128)}), f32[16,64,2,128]{3,2,1,0:T(2,128)S(1)}, u32[]{:S(2)}, u32[]{:S(2)}) async-start(f32[16,64,2,128]{3,2,1,0:T(2,128)} %copy.23), calls=%async_computation | async-start | bytes 2097152 | tf_op jit(solution)/shard_map/all_to_all | solution.py:16
  203.0 17.7 %all-to-all-done = f32[16,64,2,128]{3,2,1,0:T(2,128)S(1)} async-done(((f32[16,64,2,128]{3,2,1,0:T(2,128)}), f32[16,64,2,128]{3,2,1,0:T(2,128)S(1)}, u32[]{:S(2)}, u32[]{:S(2)}) %all-to-all-start) | async-done | bytes 1048608 | tf_op jit(solution)/shard_map/all_to_all | solution.py:16
  220.7 0.4 reduce_sum.27
  221.1 0.2 add_reduce_fusion
  221.3 0.6 broadcast_in_dim.66
  221.9 3.5 %all-to-all-start.1 = ((f32[16,1,32]{2,1,0:T(1,128)}), f32[16,1,32]{2,1,0:T(1,128)S(1)}, u32[]{:S(2)}, u32[]{:S(2)}) async-start(f32[16,1,32]{2,1,0:T(1,128)} %broadcast_in_dim.66), calls=%async_computation.1 | async-start | bytes 16384 | tf_op jit(solution)/shard_map/all_to_all | solution.py:31
  225.4 7.4 %all-to-all-done.1 = f32[16,1,32]{2,1,0:T(1,128)S(1)} async-done(((f32[16,1,32]{2,1,0:T(1,128)}), f32[16,1,32]{2,1,0:T(1,128)S(1)}, u32[]{:S(2)}, u32[]{:S(2)}) %all-to-all-start.1) | async-done | bytes 2080 | tf_op jit(solution)/shard_map/all_to_all | solution.py:31
  232.9 0.1 copy.28
  233.0 13.3 %all_gather.3 = f32[256,257]{1,0:T(8,128)S(1)} all-gather(f32[32,257]{1,0:T(8,128)S(1)} %pad_maximum_fusion.7), channel_id=1, replica_groups=mesh['tm'=16,'port'=8] {'port'}, dimensions={0}, use_global_device_ids=true | all-gather | bytes 296064 | tf_op jit(solution)/shard_map/all_gather | solution.py:44
  246.3 0.1 slice_reduce_fusion
  246.5 0.6 gather_fusion.1
  247.0 0.6 gather_fusion.2
  247.6 0.7 gather_fusion
  248.3 0.1 divide_bitcast_fusion.1
  248.4 0.6 pad_maximum_fusion.8
  (24 shorter events, 0.3 us)
Async XLA Ops:
  3.4 199.6 %copy-start = (f32[32]{0:T(128)S(1)}, f32[32]{0:T(128)}, u32[]{:S(2)}) copy-start(f32[32]{0:T(128)} %param.12) | copy-start | bytes 388
  3.4 199.6 %copy-start.1 = (s32[32]{0:T(128)S(1)}, s32[32]{0:T(128)}, u32[]{:S(2)}) copy-start(s32[32]{0:T(128)} %param.15) | copy-start | bytes 388
  194.8 25.9 %all-to-all-start = ((f32[16,64,2,128]{3,2,1,0:T(2,128)}), f32[16,64,2,128]{3,2,1,0:T(2,128)S(1)}, u32[]{:S(2)}, u32[]{:S(2)}) async-start(f32[16,64,2,128]{3,2,1,0:T(2,128)} %copy.23), calls=%async_computation | async-start | bytes 2097152 | tf_op jit(solution)/shard_map/all_to_all | solution.py:16
  221.9 10.9 %all-to-all-start.1 = ((f32[16,1,32]{2,1,0:T(1,128)}), f32[16,1,32]{2,1,0:T(1,128)S(1)}, u32[]{:S(2)}, u32[]{:S(2)}) async-start(f32[16,1,32]{2,1,0:T(1,128)} %broadcast_in_dim.66), calls=%async_computation.1 | async-start | bytes 16384 | tf_op jit(solution)/shard_map/all_to_all | solution.py:31
where the time goes:
time: 251 us; the launch traced here: 249 us
  matrix products  102 us (41%)
  other arithmetic  92.5 us (37%)
  waiting for transfers between devices  25.1 us (10%)
  blocking collectives  13.3 us (5%)
  starting transfers between devices  11.6 us (5%)
  local copies, waits for them, and re-layouts  4.41 us (2%)
    convert_element_type x4, other arithmetic, accumulate(): cos_part = (turn_cos[:, None, :] * base_cos[None] - turn_sin[:, None, :]...  61.5 us
    dot_general x4, matrix products, accumulate(): jnp.dot(part_v, table, preferred_element_type=jnp.float32)  50.8 us
    dot_general x4, matrix products, accumulate(): jnp.dot(part_c, table, preferred_element_type=jnp.float32)  50.8 us
    cos x8, other arithmetic, angles(): return (jnp.cos(angle), jnp.sin(angle))  23.2 us
    all_to_all x1, waiting for transfers between devices, summed_on_arrival(): parts = lax.all_to_all(in_blocks(shard, dim, size), axis, 0, 0, tiled=True)  17.7 us
    all_gather x1, blocking collectives, side_by_side(): result = lax.all_gather(both, axis, axis=dim, tiled=True)  13.3 us
    all_to_all x1, starting transfers between devices, summed_on_arrival(): parts = lax.all_to_all(in_blocks(shard, dim, size), axis, 0, 0, tiled=True)  8.16 us
    all_to_all x1, waiting for transfers between devices, from_everyone(): return lax.all_to_all(copies, axis, split_axis=0, concat_axis=0, tiled=True)  7.44 us
  transfers between devices with their start and end apart: 2, of which 2 were waited for; matrix products, arithmetic and copies ran while one was open for 0% of the time, Pallas kernels for 0%

commit v1 on v0

v1 whole, which is shorter than its diff:
```python
import functools
import math

import jax
import jax.numpy as jnp
from jax import lax
from jax.experimental import pallas as pl
from jax.experimental.pallas import tpu as pltpu
from jax.sharding import PartitionSpec as P

LANES = 128
COLUMNS = 256


def turned(phase, total):
    bits = total.bit_length() - 1
    wrapped = phase & (total - 1)
    quarter = (wrapped + total // 8) >> (bits - 2)
    rest = wrapped - (quarter << (bits - 2))
    x = rest.astype(jnp.float32) * (2.0 * math.pi / total)
    y = x * x
    sine = x + x * y * (-1.6666654611e-1 + y * (8.3321608736e-3 - y * 1.9515295891e-4))
    cosine = (
        1.0
        - 0.5 * y
        + y * y * (4.166664568298827e-2 + y * (-1.388731625493765e-3 + y * 2.443315711809948e-5))
    )
    odd = (quarter & 1) == 1
    even_part = jnp.where(odd, sine, cosine)
    odd_part = jnp.where(odd, cosine, sine)
    flip = ((quarter + 1) & 2) == 2
    below = (quarter & 2) == 2
    return jnp.where(flip, -even_part, even_part), jnp.where(below, odd_part, -odd_part)


def as_column(scalars, rows, dtype):
    row = lax.broadcasted_iota(jnp.int32, (rows, LANES), 0)
    column = jnp.zeros((rows, LANES), dtype)
    for r in range(rows):
        column = jnp.where(row == r, scalars[r], column)
    return column


def transform_body(
    first_ref, start_ref, lines_ref, v_ref, c_ref, out_ref, rows_ref, table_ref, *, inner, total
):
    ports, times = v_ref.shape
    both = 2 * ports
    outer = times // inner
    width = lines_ref.shape[1]

    @pl.when(pl.program_id(0) == 0)
    def _():
        start = as_column(start_ref, ports, jnp.int32)[:, :1]
        for s in range(outer):
            at = slice(s * inner, (s + 1) * inner)
            time = first_ref[0] + s * inner + lax.broadcasted_iota(jnp.int32, (ports, inner), 1)
            keep = time >= start
            low = s * both
            rows_ref[low : low + ports] = jnp.where(keep, v_ref[:, at], 0.0).astype(jnp.bfloat16)
            rows_ref[low + ports : low + both] = jnp.where(keep, c_ref[:, at], 0.0).astype(
                jnp.bfloat16
            )

    lines = lines_ref[...]

    def steps(count):
        return lax.broadcasted_iota(jnp.int32, (count, width), 0)

    fine = 16
    coarse = inner // fine
    fine_cos, fine_sin = turned(lines * steps(fine), total)
    coarse_cos, coarse_sin = turned(lines * (steps(coarse) * fine), total)
    outer_cos, outer_sin = turned(lines * (first_ref[0] + steps(outer) * inner), total)
    for u in range(coarse):
        cos_u, sin_u = coarse_cos[u : u + 1], coarse_sin[u : u + 1]
        at = slice(u * fine, (u + 1) * fine)
        table_ref[at, :width] = (cos_u * fine_cos - sin_u * fine_sin).astype(jnp.bfloat16)
        table_ref[at, width:] = (sin_u * fine_cos + cos_u * fine_sin).astype(jnp.bfloat16)
    group = max(1, 512 // both)
    re = jnp.zeros((both, width), jnp.float32)
    im = jnp.zeros((both, width), jnp.float32)
    for g in range(0, outer, group):
        part = jnp.dot(
            rows_ref[g * both : (g + group) * both],
            table_ref[...],
            preferred_element_type=jnp.float32,
        )
        for s in range(group):
            part_re = part[s * both : (s + 1) * both, :width]
            part_im = part[s * both : (s + 1) * both, width:]
            cos_s, sin_s = outer_cos[g + s : g + s + 1], outer_sin[g + s : g + s + 1]
            re = re + (part_re * cos_s - part_im * sin_s)
            im = im + (part_re * sin_s + part_im * cos_s)
    for d in range(width // LANES):
        at = slice(d * LANES, (d + 1) * LANES)
        out_ref[d, :both] = re[:, at]
        out_ref[d, both:] = im[:, at]


def transform(first, start, freq_index, voltages, currents, total):
    ports, times = voltages.shape
    count = freq_index.shape[0]
    inner = min(times, 1024)
    width = min(count, COLUMNS)
    held = pl.BlockSpec((ports, times), lambda i: (0, 0), pipeline_mode=pl.Buffered(1))
    return pl.pallas_call(
        functools.partial(transform_body, inner=inner, total=total),
        grid=(count // width,),
        in_specs=[
            pl.BlockSpec(memory_space=pltpu.SMEM),
            pl.BlockSpec(memory_space=pltpu.SMEM),
            pl.BlockSpec((1, width), lambda i: (0, i)),
            held,
            held,
        ],
        out_specs=pl.BlockSpec((width // LANES, 4 * ports, LANES), lambda i: (i, 0, 0)),
        out_shape=jax.ShapeDtypeStruct((count // LANES, 4 * ports, LANES), jnp.float32),
        scratch_shapes=[
            pltpu.VMEM((times // inner * 2 * ports, inner), jnp.bfloat16),
            pltpu.VMEM((inner, 2 * width), jnp.bfloat16),
        ],
        compiler_params=pltpu.CompilerParams(
            dimension_semantics=("arbitrary",), vmem_limit_bytes=48 << 20
        ),
        name="transform",
    )(first.reshape(1), start, freq_index.reshape(1, count), voltages, currents)


def waves_body(impedance_ref, parts_ref, sent_ref, own_ref, *, scale):
    ports = own_ref.shape[0]
    total = jnp.sum(parts_ref[...], axis=0) * scale
    z = as_column(impedance_ref, ports, jnp.float32)
    inverse = 1.0 / (2.0 * jnp.sqrt(z))
    v_re, c_re = total[:ports], total[ports : 2 * ports]
    v_im, c_im = total[2 * ports : 3 * ports], total[3 * ports :]
    a = jnp.concatenate([(v_re + z * c_re) * inverse, (v_im + z * c_im) * inverse], axis=1)
    own_ref[:, :LANES] = (v_re - z * c_re) * inverse
    own_ref[:, LANES:] = (v_im - z * c_im) * inverse
    for d in range(sent_ref.shape[0]):
        sent_ref[d] = a


def pick_body(pairing_ref, every_ref, own_ref, sent_ref, out_ref, q_ref):
    ports = own_ref.shape[0]
    for p in range(ports):
        q_ref[p : p + 1] = every_ref[pl.ds(pairing_ref[p], 1)]
    q_re, q_im = q_ref[:, :LANES], q_ref[:, LANES:]
    b_re, b_im = own_ref[:, :LANES], own_ref[:, LANES:]
    power = q_re * q_re + q_im * q_im
    out_ref[0] = b_re * q_re + b_im * q_im
    out_ref[1] = b_im * q_re - b_re * q_im
    out_ref[2] = power
    padded = jnp.concatenate([power, jnp.zeros((LANES - ports, LANES), jnp.float32)], axis=0)
    share = jnp.sum(padded.T, axis=0, keepdims=True)
    for d in range(sent_ref.shape[0]):
        sent_ref[d] = jnp.broadcast_to(share, sent_ref.shape[1:])


def divide_body(shares_ref, made_ref, out_ref, *, width):
    ports = out_ref.shape[1]
    summed = jnp.sum(shares_ref[:, 0, :], axis=0, keepdims=True)
    mean = jnp.broadcast_to(summed / width + 1e-06, (LANES, LANES)).T[:ports]
    inverse = 1.0 / jnp.maximum(made_ref[2], 0.1 * mean)
    out_ref[0] = made_ref[0] * inverse
    out_ref[1] = made_ref[1] * inverse


def body(voltages, currents, impedance, freq_index, window_start, pairing):
    ports, times = voltages.shape
    width = freq_index.shape[0]
    times_count, ports_count = lax.axis_size("tm"), lax.axis_size("port")
    total = times * times_count
    first = lax.axis_index("tm") * times
    parts = transform(first, window_start, freq_index, voltages, currents, total)
    parts = lax.all_to_all(parts, "tm", 0, 0, tiled=True)
    smem = pl.BlockSpec(memory_space=pltpu.SMEM)
    vmem = pl.BlockSpec(memory_space=pltpu.VMEM)
    sent, own = pl.pallas_call(
        functools.partial(waves_body, scale=1.0 / math.sqrt(total)),
        in_specs=[smem, vmem],
        out_specs=[vmem, vmem],
        out_shape=[
            jax.ShapeDtypeStruct((ports_count, ports, 2 * LANES), jnp.float32),
            jax.ShapeDtypeStruct((ports, 2 * LANES), jnp.float32),
        ],
        name="waves",
    )(impedance, parts)
    every = lax.all_to_all(sent, "port", 0, 0, tiled=True)
    every = every.reshape(ports_count * ports, 2 * LANES)
    shares, made = pl.pallas_call(
        pick_body,
        in_specs=[smem, vmem, vmem],
        out_specs=[vmem, vmem],
        out_shape=[
            jax.ShapeDtypeStruct((times_count, 8, LANES), jnp.float32),
            jax.ShapeDtypeStruct((3, ports, LANES), jnp.float32),
        ],
        scratch_shapes=[pltpu.VMEM((ports, 2 * LANES), jnp.float32)],
        name="pick",
    )(pairing, every, own)
    shares = lax.all_to_all(shares, "tm", 0, 0, tiled=True)
    return pl.pallas_call(
        functools.partial(divide_body, width=width),
        in_specs=[vmem, vmem],
        out_specs=vmem,
        out_shape=jax.ShapeDtypeStruct((2, ports, LANES), jnp.float32),
        name="divide",
    )(shares, made)


def solution(mesh):
    placed = (P("port", "tm"), P("port", "tm"), P("port"), P(), P("port"), P("port"))
    return jax.shard_map(
        body, mesh=mesh, in_specs=placed, out_specs=P(None, "port", "tm"), check_vma=False
    )
```

time: 251 us -> 71 us (0.28)
  matrix products: 102 us -> 0 us
  other arithmetic: 92.5 us -> 0 us
  blocking collectives: 13.3 us -> 48.6 us
  waiting for transfers between devices: 25.1 us -> 0 us
  Pallas kernels: 0 us -> 17.3 us
  starting transfers between devices: 11.6 us -> 0 us
    dot_general x8 -> x0, matrix products: 102 us -> none  [the longest x4 50.8 us: accumulate(): jnp.dot(part_v, table, preferred_element_type=jnp.float32)]
    convert_element_type x5 -> x0, other arithmetic: 64.1 us -> none  [the longest x4 61.5 us: accumulate(): cos_part = (turn_cos[:, None, :] * base_cos[None] - turn_sin[:, None, :]...]
    all_to_all x0 -> x3, blocking collectives: none -> 48.6 us  [the longest x1 24.9 us: body(): parts = lax.all_to_all(parts, 'tm', 0, 0, tiled=True)]
    all_to_all x2 -> x0, waiting for transfers between devices: 25.1 us -> none  [the longest x1 17.7 us: summed_on_arrival(): parts = lax.all_to_all(in_blocks(shard, dim, size), axis, 0, 0, tiled=True)]
    cos x8 -> x0, other arithmetic: 23.2 us -> none  [angles(): return (jnp.cos(angle), jnp.sin(angle))]
    pallas_call x0 -> x4, Pallas kernels: none -> 17.3 us  [the longest x1 12 us: transform(): pl.pallas_call(functools.partial(transform_body, inner=inner, total=total...]
    all_gather x1 -> x0, blocking collectives: 13.3 us -> none  [side_by_side(): result = lax.all_gather(both, axis, axis=dim, tiled=True)]
    all_to_all x2 -> x0, starting transfers between devices: 11.6 us -> none  [the longest x1 8.16 us: summed_on_arrival(): parts = lax.all_to_all(in_blocks(shard, dim, size), axis, 0, 0, tiled=True)]
  transfers between devices with their start and end apart: 2 -> 0, of which waited for: 2 -> 0; matrix products, arithmetic and copies ran while one was open for 0% -> 0% of each run, Pallas kernels for 0% -> 0%
where the time goes in v1:
time: 71 us; the launch traced here: 70.5 us
  blocking collectives  48.6 us (68%)
  Pallas kernels  17.3 us (24%)
  local copies, waits for them, and re-layouts  4.53 us (6%)
    all_to_all x1, blocking collectives, body(): parts = lax.all_to_all(parts, 'tm', 0, 0, tiled=True)  24.9 us
    pallas_call x1, Pallas kernels, transform(): pl.pallas_call(functools.partial(transform_body, inner=inner, total=total...  12 us
    all_to_all x1, blocking collectives, body(): every = lax.all_to_all(sent, 'port', 0, 0, tiled=True)  11.9 us
    all_to_all x1, blocking collectives, body(): shares = lax.all_to_all(shares, 'tm', 0, 0, tiled=True)  11.8 us
    unnamed x8, local copies, waits for them, and re-layouts  4.53 us
    pallas_call x1, Pallas kernels, body(): pl.pallas_call(functools.partial(waves_body, scale=1.0 / math.sqrt(total)...  2.01 us
    pallas_call x1, Pallas kernels, body(): pl.pallas_call(pick_body, in_specs=[smem, vmem, vmem], out_specs=[vmem, v...  1.75 us
    pallas_call x1, Pallas kernels, body(): pl.pallas_call(functools.partial(divide_body, width=width), in_specs=[vme...  1.56 us

profile of v1, /device:TPU:0, one launch (start us, length us, event | category | flops | bytes accessed | tf_op | source)
XLA Modules:
  0.0 70.5 jit_solution(12153544643280346159)
XLA Ops:
  0.0 0.0 copy-start
  0.0 1.6 %copy-done = f32[32,16384]{1,0:T(8,128)S(1)} copy-done((f32[32,16384]{1,0:T(8,128)S(1)}, f32[32,16384]{1,0:T(8,128)}, u32[]{:S(2)}) %copy-start) | copy-done | bytes 2097176
  1.6 0.0 copy-start.1
  1.6 1.6 %copy-done.1 = f32[32,16384]{1,0:T(8,128)S(1)} copy-done((f32[32,16384]{1,0:T(8,128)S(1)}, f32[32,16384]{1,0:T(8,128)}, u32[]{:S(2)}) %copy-start.1) | copy-done | bytes 2097176
  3.2 0.0 copy-start.2
  3.2 0.7 copy-done.2
  3.9 0.0 copy-start.3
  3.9 0.7 copy-done.3
  4.5 12.0 %transform.1 = f32[16,128,128]{2,1,0:T(8,128)S(1)} custom-call(s32[1]{0:T(128)} %bitcast.first_ref, s32[32]{0:T(128)S(1)} %copy-done.3, s32[1,2048]{1,0:T(1,128)S(1)} %bitcast.3, f32[32,16384]{1,0:T(8,128)S(1)} %copy-done, f32[32,16384]{1,0:T(8,128)S(1)} %copy-done.1), custom_call_target="tpu_custom_call" | custom-call | tf_op jit(solution)/shard_map/transform/pallas_call | solution.py:107
  16.5 24.9 %all_to_all.15.parts_ref = f32[16,128,128]{2,1,0:T(8,128)} all-to-all(f32[16,128,128]{2,1,0:T(8,128)S(1)} %transform.1), channel_id=1, replica_groups=mesh['tm'=16,'port'=8] {'tm'}, dimensions={0} | all-to-all | bytes 2097152 | tf_op jit(solution)/shard_map/all_to_all | solution.py:176
  41.4 2.0 %waves.1 = (f32[8,32,256]{2,1,0:T(8,128)}, f32[32,256]{1,0:T(8,128)}) custom-call(f32[32]{0:T(128)} %impedance_ref.1, f32[16,128,128]{2,1,0:T(8,128)} %all_to_all.15.parts_ref), custom_call_target="tpu_custom_call" | custom-call | tf_op jit(solution)/shard_map/waves/pallas_call | solution.py:179
  43.5 11.9 %all_to_all.16 = f32[8,32,256]{2,1,0:T(8,128)} all-to-all(f32[8,32,256]{2,1,0:T(8,128)} %get-tuple-element.9), channel_id=1, replica_groups=mesh['tm'=16,'port'=8] {'port'}, dimensions={0} | all-to-all | bytes 524288 | tf_op jit(solution)/shard_map/all_to_all | solution.py:189
  55.4 1.8 %pick.1 = (f32[16,8,128]{2,1,0:T(8,128)}, f32[3,32,128]{2,1,0:T(8,128)}) custom-call(s32[32]{0:T(128)} %pairing_ref.1, f32[256,256]{1,0:T(8,128)} %bitcast.4, f32[32,256]{1,0:T(8,128)} %get-tuple-element.10.own_ref), custom_call_target="tpu_custom_call" | custom-call | tf_op jit(solution)/shard_map/pick/pallas_call | solution.py:191
  57.1 11.8 %all_to_all.17.shares_ref = f32[16,8,128]{2,1,0:T(8,128)} all-to-all(f32[16,8,128]{2,1,0:T(8,128)} %get-tuple-element.11), channel_id=1, replica_groups=mesh['tm'=16,'port'=8] {'tm'}, dimensions={0} | all-to-all | bytes 131072 | tf_op jit(solution)/shard_map/all_to_all | solution.py:202
  68.9 1.6 %divide.1 = f32[2,32,128]{2,1,0:T(8,128)} custom-call(f32[16,8,128]{2,1,0:T(8,128)} %all_to_all.17.shares_ref, f32[3,32,128]{2,1,0:T(8,128)} %get-tuple-element.12.made_ref), custom_call_target="tpu_custom_call" | custom-call | tf_op jit(solution)/shard_map/divide/pallas_call | solution.py:203
Async XLA Ops:
  0.0 1.6 %copy-start = (f32[32,16384]{1,0:T(8,128)S(1)}, f32[32,16384]{1,0:T(8,128)}, u32[]{:S(2)}) copy-start(f32[32,16384]{1,0:T(8,128)} %v_ref.1) | copy-start | bytes 6291460
  1.6 1.6 %copy-start.1 = (f32[32,16384]{1,0:T(8,128)S(1)}, f32[32,16384]{1,0:T(8,128)}, u32[]{:S(2)}) copy-start(f32[32,16384]{1,0:T(8,128)} %c_ref.1) | copy-start | bytes 6291460
  3.2 0.7 copy-start.2
  3.9 0.7 copy-start.3

commit v2 on v1

v2 whole, which is shorter than its diff:
```python
import functools
import math

import jax
import jax.numpy as jnp
from jax import lax
from jax.experimental import pallas as pl
from jax.experimental.pallas import tpu as pltpu
from jax.sharding import PartitionSpec as P


LANES = 128
HALF = LANES // 2
COLUMNS = 256
INNER = 1024
SMEM = pl.BlockSpec(memory_space=pltpu.SMEM)
VMEM = pl.BlockSpec(memory_space=pltpu.VMEM)
HBM = pl.BlockSpec(memory_space=pltpu.HBM)


def in_hbm(array):
    return pltpu.with_memory_space_constraint(array, pltpu.HBM)


def in_vmem(array):
    return pltpu.with_memory_space_constraint(array, pltpu.VMEM)


def turned(phase, total):
    bits = total.bit_length() - 1
    wrapped = phase & (total - 1)
    quarter = (wrapped + total // 8) >> (bits - 2)
    rest = wrapped - (quarter << (bits - 2))
    x = rest.astype(jnp.float32) * (2.0 * math.pi / total)
    y = x * x
    sine = x + x * y * (-1.6666654611e-1 + y * (8.3321608736e-3 - y * 1.9515295891e-4))
    cosine = (
        1.0
        - 0.5 * y
        + y * y * (4.166664568298827e-2 + y * (-1.388731625493765e-3 + y * 2.443315711809948e-5))
    )
    odd = (quarter & 1) == 1
    even_part = jnp.where(odd, sine, cosine)
    odd_part = jnp.where(odd, cosine, sine)
    flip = ((quarter + 1) & 2) == 2
    below = (quarter & 2) == 2
    return jnp.where(flip, -even_part, even_part), jnp.where(below, odd_part, -odd_part)


def as_column(scalars, rows, dtype):
    row = lax.broadcasted_iota(jnp.int32, (rows, LANES), 0)
    column = jnp.zeros((rows, LANES), dtype)
    for r in range(rows):
        column = jnp.where(row == r, scalars[r], column)
    return column


def lower(shape):
    return lax.broadcasted_iota(jnp.int32, shape, 1) < HALF


def joined(first, second, which):
    if which == 0:
        return jnp.where(lower(first.shape), first, pltpu.roll(second, HALF, 1))
    return jnp.where(lower(first.shape), pltpu.roll(first, HALF, 1), second)


def add_lines(first_ref, lines_ref, rows_ref, table_ref, out_ref, *, both, inner, total, which):
    outer = rows_ref.shape[0] // both
    tiles = lines_ref.shape[1] // (2 * LANES)
    width = tiles * LANES
    lines = jnp.concatenate(
        [
            joined(
                lines_ref[:, 2 * j * LANES : (2 * j + 1) * LANES],
                lines_ref[:, (2 * j + 1) * LANES : (2 * j + 2) * LANES],
                which,
            )
            for j in range(tiles)
        ],
        axis=1,
    )

    def steps(count):
        return lax.broadcasted_iota(jnp.int32, (count, width), 0)

    fine = 16
    coarse = inner // fine
    fine_cos, fine_sin = turned(lines * steps(fine), total)
    coarse_cos, coarse_sin = turned(lines * (steps(coarse) * fine), total)
    outer_cos, outer_sin = turned(lines * (first_ref[0] + steps(outer) * inner), total)
    for u in range(coarse):
        cos_u, sin_u = coarse_cos[u : u + 1], coarse_sin[u : u + 1]
        at = slice(u * fine, (u + 1) * fine)
        table_ref[at, :width] = (cos_u * fine_cos - sin_u * fine_sin).astype(jnp.bfloat16)
        table_ref[at, width:] = (sin_u * fine_cos + cos_u * fine_sin).astype(jnp.bfloat16)
    yield
    group = max(1, 512 // both)
    re = jnp.zeros((both, width), jnp.float32)
    im = jnp.zeros((both, width), jnp.float32)
    for g in range(0, outer, group):
        part = jnp.dot(
            rows_ref[g * both : (g + group) * both],
            table_ref[...],
            preferred_element_type=jnp.float32,
        )
        for s in range(group):
            part_re = part[s * both : (s + 1) * both, :width]
            part_im = part[s * both : (s + 1) * both, width:]
            cos_s, sin_s = outer_cos[g + s : g + s + 1], outer_sin[g + s : g + s + 1]
            re = re + (part_re * cos_s - part_im * sin_s)
            im = im + (part_re * sin_s + part_im * cos_s)
    for j in range(tiles):
        at = slice(j * LANES, (j + 1) * LANES)
        for h in range(2):
            out_ref[2 * j + h] = joined(re[:, at], im[:, at], h)
    yield


def first_body(
    first_ref, start_ref, lines_ref, v_ref, c_ref, out_ref, rows_ref, table_ref, v_in, c_in, sems,
    *, inner, total
):
    ports, times = v_in.shape
    both = 2 * ports
    outer = times // inner
    begin = pl.program_id(0) == 0

    def copies(s):
        at = pl.ds(s * inner, inner)
        return (
            pltpu.make_async_copy(v_ref.at[:, at], v_in.at[:, at], sems.at[0, s]),
            pltpu.make_async_copy(c_ref.at[:, at], c_in.at[:, at], sems.at[1, s]),
        )

    @pl.when(begin)
    def _():
        for s in range(outer):
            for copy in copies(s):
                copy.start()

    work = add_lines(
        first_ref, lines_ref, rows_ref, table_ref, out_ref,
        both=both, inner=inner, total=total, which=0,
    )
    next(work)

    @pl.when(begin)
    def _():
        start = as_column(start_ref, ports, jnp.int32)[:, :1]
        for s in range(outer):
            at = slice(s * inner, (s + 1) * inner)
            time = first_ref[0] + s * inner + lax.broadcasted_iota(jnp.int32, (ports, inner), 1)
            keep = time >= start
            low = s * both
            for copy in copies(s):
                copy.wait()
            rows_ref[low : low + ports] = jnp.where(keep, v_in[:, at], 0.0).astype(jnp.bfloat16)
            rows_ref[low + ports : low + both] = jnp.where(keep, c_in[:, at], 0.0).astype(
                jnp.bfloat16
            )

    next(work)


def second_body(first_ref, lines_ref, rows_ref, out_ref, table_ref, *, both, inner, total):
    work = add_lines(
        first_ref, lines_ref, rows_ref, table_ref, out_ref,
        both=both, inner=inner, total=total, which=1,
    )
    next(work)
    next(work)


def transforms(first, start, freq_index, voltages, currents, total):
    ports, times = voltages.shape
    both = 2 * ports
    count = freq_index.shape[0]
    inner = min(times, INNER)
    outer = times // inner
    lines = pl.BlockSpec((1, 2 * COLUMNS), lambda i: (0, i))
    grid = (count // (2 * COLUMNS),)
    out_spec = pl.BlockSpec((2 * COLUMNS // LANES, both, LANES), lambda i: (i, 0, 0))
    out_shape = pltpu.VMEM((count // LANES, both, LANES), jnp.float32)
    rows_spec = pl.BlockSpec((outer * both, inner), lambda i: (0, 0), pipeline_mode=pl.Buffered(1))
    rows_shape = pltpu.VMEM((outer * both, inner), jnp.bfloat16)
    table = pltpu.VMEM((inner, 2 * COLUMNS), jnp.bfloat16)
    params = pltpu.CompilerParams(dimension_semantics=("arbitrary",), vmem_limit_bytes=40 << 20)
    cost = pl.CostEstimate(
        flops=2 * both * times * count, transcendentals=0, bytes_accessed=8 * ports * times
    )
    first = first.reshape(1)
    freq_index = freq_index.reshape(1, count)
    out_0, rows = pl.pallas_call(
        functools.partial(first_body, inner=inner, total=total),
        grid=grid,
        in_specs=[SMEM, SMEM, lines, HBM, HBM],
        out_specs=[out_spec, rows_spec],
        out_shape=[out_shape, rows_shape],
        scratch_shapes=[
            table,
            pltpu.VMEM((ports, times), jnp.float32),
            pltpu.VMEM((ports, times), jnp.float32),
            pltpu.SemaphoreType.DMA((2, outer)),
        ],
        compiler_params=params,
        cost_estimate=cost,
        name="spectrum_first",
    )(first, in_hbm(start), in_hbm(freq_index), in_hbm(voltages), in_hbm(currents))
    out_1 = pl.pallas_call(
        functools.partial(second_body, both=both, inner=inner, total=total),
        grid=grid,
        in_specs=[SMEM, lines, rows_spec],
        out_specs=out_spec,
        out_shape=out_shape,
        scratch_shapes=[table],
        compiler_params=params,
        cost_estimate=cost,
        name="spectrum_second",
    )(first, in_hbm(freq_index), in_vmem(rows))
    return out_0, out_1


def waves_body(impedance_ref, parts_ref, sent_ref, own_ref, *, scale):
    ports = own_ref.shape[0]
    total = jnp.sum(parts_ref[...], axis=0) * scale
    z = as_column(impedance_ref, ports, jnp.float32)
    inverse = 1.0 / (2.0 * jnp.sqrt(z))
    v, c = total[:ports], total[ports:]
    a = (v + z * c) * inverse
    own_ref[...] = (v - z * c) * inverse
    for d in range(sent_ref.shape[0]):
        sent_ref[d] = a


def waves(impedance, parts, total, ports_count):
    ports = parts.shape[1] // 2
    return pl.pallas_call(
        functools.partial(waves_body, scale=1.0 / math.sqrt(total)),
        in_specs=[SMEM, VMEM],
        out_specs=[VMEM, VMEM],
        out_shape=[
            pltpu.VMEM((ports_count, ports, LANES), jnp.float32),
            pltpu.VMEM((ports, LANES), jnp.float32),
        ],
        name="waves",
    )(in_hbm(impedance), in_vmem(parts))


def pick_body(pairing_ref, every_0, every_1, own_0, own_1, sent_ref, out_ref, q_ref):
    ports = own_0.shape[0]
    summed = jnp.zeros((ports, LANES), jnp.float32)
    for h, (every_ref, own_ref) in enumerate(((every_0, own_0), (every_1, own_1))):
        for p in range(ports):
            q_ref[h, p : p + 1] = every_ref[pl.ds(pairing_ref[p], 1)]
        q, b = q_ref[h], own_ref[...]
        square = q * q
        summed = summed + square
        same = b * q
        cross = b * pltpu.roll(q, HALF, 1)
        out_ref[h, 0] = jnp.where(
            lower(q.shape), same + pltpu.roll(same, HALF, 1), cross - pltpu.roll(cross, HALF, 1)
        )
        out_ref[h, 1] = square + pltpu.roll(square, HALF, 1)
    padded = jnp.concatenate([summed, jnp.zeros((LANES - ports, LANES), jnp.float32)], axis=0)
    share = jnp.sum(padded.T, axis=0, keepdims=True)
    sent_ref[...] = jnp.broadcast_to(share, sent_ref.shape)


def divide_body(shares_ref, made_ref, out_ref, *, width):
    ports = out_ref.shape[1]
    summed = jnp.sum(shares_ref[...], axis=0, keepdims=True)
    mean = jnp.broadcast_to(summed / width + 1e-06, (LANES, LANES)).T[:ports]
    halves = [made_ref[h, 0] / jnp.maximum(made_ref[h, 1], 0.1 * mean) for h in range(2)]
    for r in range(2):
        out_ref[r] = joined(halves[0], halves[1], r)


def body(voltages, currents, impedance, freq_index, window_start, pairing):
    ports, times = voltages.shape
    width = freq_index.shape[0]
    times_count, ports_count = lax.axis_size("tm"), lax.axis_size("port")
    total = times * times_count
    first = lax.axis_index("tm") * times
    everyone, own = [], []
    halves = transforms(first, window_start, freq_index, voltages, currents, total)
    for parts in halves:
        parts = lax.all_to_all(in_vmem(parts), "tm", 0, 0, tiled=True)
        sent, mine = waves(impedance, parts, total, ports_count)
        every = lax.all_to_all(sent, "port", 0, 0, tiled=True)
        everyone.append(every.reshape(ports_count * ports, LANES))
        own.append(mine)
    shares, made = pl.pallas_call(
        pick_body,
        in_specs=[SMEM, VMEM, VMEM, VMEM, VMEM],
        out_specs=[VMEM, VMEM],
        out_shape=[
            pltpu.VMEM((times_count, LANES), jnp.float32),
            pltpu.VMEM((2, 2, ports, LANES), jnp.float32),
        ],
        scratch_shapes=[pltpu.VMEM((2, ports, LANES), jnp.float32)],
        name="pick",
    )(in_hbm(pairing), *map(in_vmem, everyone), *map(in_vmem, own))
    shares = lax.all_to_all(shares, "tm", 0, 0, tiled=True)
    return pl.pallas_call(
        functools.partial(divide_body, width=width),
        in_specs=[VMEM, VMEM],
        out_specs=VMEM,
        out_shape=jax.ShapeDtypeStruct((2, ports, LANES), jnp.float32),
        name="divide",
    )(in_vmem(shares), in_vmem(made))


def solution(mesh):
    placed = (P("port", "tm"), P("port", "tm"), P("port"), P(), P("port"), P("port"))
    return jax.shard_map(
        body, mesh=mesh, in_specs=placed, out_specs=P(None, "port", "tm"), check_vma=False
    )
```

time: 71 us -> 83.3 us (1.17)
  waiting for transfers between devices: 0 us -> 14.4 us
  blocking collectives: 48.6 us -> 38.8 us
  starting transfers between devices: 0 us -> 7.87 us
  local copies, waits for them, and re-layouts: 4.53 us -> 0 us
  Pallas kernels: 17.3 us -> 21.7 us
    all_to_all x0 -> x2, waiting for transfers between devices: none -> 14.4 us  [the longest x1 8.97 us: body(): parts = lax.all_to_all(in_vmem(parts), 'tm', 0, 0, tiled=True)]
    all_to_all x0 -> x2, starting transfers between devices: none -> 7.87 us  [the longest x1 4.3 us: body(): every = lax.all_to_all(sent, 'port', 0, 0, tiled=True)]
    all_to_all x1, blocking collectives: 24.9 us -> 19.4 us  [body(): parts = lax.all_to_all(in_vmem(parts), 'tm', 0, 0, tiled=True)]
    unnamed x8 -> x0, local copies, waits for them, and re-layouts: 4.53 us -> none
    pallas_call x4 -> x6, Pallas kernels: 17.3 us -> 21.7 us  [the longest x1 10.9 us: transforms(): pl.pallas_call(functools.partial(first_body, inner=inner, total=total), g...]
    all_to_all x1, blocking collectives: 11.9 us -> 8.48 us  [body(): every = lax.all_to_all(sent, 'port', 0, 0, tiled=True)]
    all_to_all x1, blocking collectives: 11.8 us -> 10.8 us  [body(): shares = lax.all_to_all(shares, 'tm', 0, 0, tiled=True)]
  transfers between devices with their start and end apart: 0 -> 2, of which waited for: 0 -> 2; matrix products, arithmetic and copies ran while one was open for 0% -> 0% of each run, Pallas kernels for 0% -> 2%
where the time goes in v2:
time: 83.3 us; the launch traced here: 82.8 us
  blocking collectives  38.8 us (47%)
  Pallas kernels  21.7 us (26%)
  waiting for transfers between devices  14.4 us (17%)
  starting transfers between devices  7.87 us (9%)
    all_to_all x1, blocking collectives, body(): parts = lax.all_to_all(in_vmem(parts), 'tm', 0, 0, tiled=True)  19.4 us
    pallas_call x1, Pallas kernels, transforms(): pl.pallas_call(functools.partial(first_body, inner=inner, total=total), g...  10.9 us
    all_to_all x1, blocking collectives, body(): shares = lax.all_to_all(shares, 'tm', 0, 0, tiled=True)  10.8 us
    all_to_all x1, waiting for transfers between devices, body(): parts = lax.all_to_all(in_vmem(parts), 'tm', 0, 0, tiled=True)  8.97 us
    all_to_all x1, blocking collectives, body(): every = lax.all_to_all(sent, 'port', 0, 0, tiled=True)  8.48 us
    pallas_call x1, Pallas kernels, transforms(): pl.pallas_call(functools.partial(second_body, both=both, inner=inner, tot...  7.11 us
    all_to_all x1, waiting for transfers between devices, body(): every = lax.all_to_all(sent, 'port', 0, 0, tiled=True)  5.38 us
    all_to_all x1, starting transfers between devices, body(): every = lax.all_to_all(sent, 'port', 0, 0, tiled=True)  4.3 us
  transfers between devices with their start and end apart: 2, of which 2 were waited for; matrix products, arithmetic and copies ran while one was open for 0% of the time, Pallas kernels for 2%

profile of v2, /device:TPU:0, one launch (start us, length us, event | category | flops | bytes accessed | tf_op | source)
XLA Modules:
  0.0 82.8 jit_solution(2485853917653495203)
XLA Ops:
  0.0 10.9 %spectrum_first.1 = (f32[16,64,128]{2,1,0:T(8,128)}, bf16[1024,1024]{1,0:T(8,128)(2,1)S(1)}) custom-call(s32[1]{0:T(128)} %bitcast.first_ref, s32[32]{0:T(128)} %start_ref.1, s32[1,2048]{1,0:T(1,128)} %bitcast.12, f32[32,16384]{1,0:T(8,128)} %v_ref.1, f32[32,16384]{1,0:T(8,128)} %c_ref.1), custom_call_target="tpu_custom_call" | custom-call | flops 4294967296 | bytes 4194304 | tf_op jit(solution)/shard_map/spectrum_first/pallas_call | solution.py:194
  11.0 7.1 %spectrum_second.1 = f32[16,64,128]{2,1,0:T(8,128)S(1)} custom-call(s32[1]{0:T(128)} %bitcast.first_ref, s32[1,2048]{1,0:T(1,128)} %bitcast.13, bf16[1024,1024]{1,0:T(8,128)(2,1)S(1)} %get-tuple-element.15.rows_ref), custom_call_target="tpu_custom_call" | custom-call | flops 4294967296 | bytes 4194304 | tf_op jit(solution)/shard_map/spectrum_second/pallas_call | solution.py:210
  18.1 19.4 %all_to_all.31.parts_ref = f32[16,64,128]{2,1,0:T(8,128)S(1)} all-to-all(f32[16,64,128]{2,1,0:T(8,128)S(1)} %spectrum_second.1), channel_id=1, replica_groups=mesh['tm'=16,'port'=8] {'tm'}, dimensions={0} | all-to-all | bytes 1048576 | tf_op jit(solution)/shard_map/all_to_all | solution.py:288
  37.5 3.6 %all-to-all-start = ((f32[16,64,128]{2,1,0:T(8,128)}), f32[16,64,128]{2,1,0:T(8,128)S(1)}, u32[]{:S(2)}, u32[]{:S(2)}) async-start(f32[16,64,128]{2,1,0:T(8,128)} %get-tuple-element.13), calls=%async_computation | async-start | bytes 1048576 | tf_op jit(solution)/shard_map/all_to_all | solution.py:288
  41.1 1.4 %waves.3 = (f32[8,32,128]{2,1,0:T(8,128)}, f32[32,128]{1,0:T(8,128)S(1)}) custom-call(f32[32]{0:T(128)} %impedance_ref.3, f32[16,64,128]{2,1,0:T(8,128)S(1)} %all_to_all.31.parts_ref), custom_call_target="tpu_custom_call" | custom-call | tf_op jit(solution)/shard_map/waves/pallas_call | solution.py:238
  42.4 9.0 %all-to-all-done.parts_ref = f32[16,64,128]{2,1,0:T(8,128)S(1)} async-done(((f32[16,64,128]{2,1,0:T(8,128)}), f32[16,64,128]{2,1,0:T(8,128)S(1)}, u32[]{:S(2)}, u32[]{:S(2)}) %all-to-all-start) | async-done | bytes 524320 | tf_op jit(solution)/shard_map/all_to_all | solution.py:288
  51.4 4.3 %all-to-all-start.3 = ((f32[8,32,128]{2,1,0:T(8,128)}), f32[8,32,128]{2,1,0:T(8,128)S(1)}, u32[]{:S(2)}, u32[]{:S(2)}) async-start(f32[8,32,128]{2,1,0:T(8,128)} %get-tuple-element.16), calls=%async_computation.3 | async-start | bytes 262144 | tf_op jit(solution)/shard_map/all_to_all | solution.py:290
  55.7 0.7 waves.2
  56.4 5.4 %all-to-all-done.3 = f32[8,32,128]{2,1,0:T(8,128)S(1)} async-done(((f32[8,32,128]{2,1,0:T(8,128)}), f32[8,32,128]{2,1,0:T(8,128)S(1)}, u32[]{:S(2)}, u32[]{:S(2)}) %all-to-all-start.3) | async-done | bytes 131104 | tf_op jit(solution)/shard_map/all_to_all | solution.py:290
  61.8 8.5 %all_to_all.32 = f32[8,32,128]{2,1,0:T(8,128)S(1)} all-to-all(f32[8,32,128]{2,1,0:T(8,128)S(1)} %get-tuple-element.14), channel_id=1, replica_groups=mesh['tm'=16,'port'=8] {'port'}, dimensions={0} | all-to-all | bytes 262144 | tf_op jit(solution)/shard_map/all_to_all | solution.py:290
  70.3 0.8 %pick.1 = (f32[16,128]{1,0:T(8,128)S(1)}, f32[2,2,32,128]{3,2,1,0:T(8,128)S(1)}) custom-call(s32[32]{0:T(128)} %pairing_ref.1, f32[256,128]{1,0:T(8,128)S(1)} %bitcast.9, f32[256,128]{1,0:T(8,128)S(1)} %bitcast.8, f32[32,128]{1,0:T(8,128)S(1)} %get-tuple-element.17.own_0, f32[32,128]{1,0:T(8,128)S(1)} %get-tuple-element.18.own_1), custom_call_target="tpu_custom_call" | custom-call | tf_op jit(solution)/shard_map/pick/pallas_call | solution.py:293
  71.2 10.8 %all_to_all.33 = f32[16,1,128]{2,1,0:T(1,128)S(1)} all-to-all(f32[16,1,128]{2,1,0:T(1,128)S(1)} %bitcast.11), channel_id=1, replica_groups=mesh['tm'=16,'port'=8] {'tm'}, dimensions={0} | all-to-all | bytes 16384 | tf_op jit(solution)/shard_map/all_to_all | solution.py:304
  82.0 0.8 divide.1
Async XLA Ops:
  37.5 13.9 %all-to-all-start = ((f32[16,64,128]{2,1,0:T(8,128)}), f32[16,64,128]{2,1,0:T(8,128)S(1)}, u32[]{:S(2)}, u32[]{:S(2)}) async-start(f32[16,64,128]{2,1,0:T(8,128)} %get-tuple-element.13), calls=%async_computation | async-start | bytes 1048576 | tf_op jit(solution)/shard_map/all_to_all | solution.py:288
  51.4 10.4 %all-to-all-start.3 = ((f32[8,32,128]{2,1,0:T(8,128)}), f32[8,32,128]{2,1,0:T(8,128)S(1)}, u32[]{:S(2)}, u32[]{:S(2)}) async-start(f32[8,32,128]{2,1,0:T(8,128)} %get-tuple-element.16), calls=%async_computation.3 | async-start | bytes 262144 | tf_op jit(solution)/shard_map/all_to_all | solution.py:290

commit v3 on v1

v3 whole, which is shorter than its diff:
```python
import functools
import math

import jax
import jax.numpy as jnp
from jax import lax
from jax.experimental import pallas as pl
from jax.experimental.pallas import tpu as pltpu
from jax.sharding import PartitionSpec as P

LANES = 128
COLUMNS = 256
INNER = 1024
FLIP = 256
SMEM = pl.BlockSpec(memory_space=pltpu.SMEM)
VMEM = pl.BlockSpec(memory_space=pltpu.VMEM)
HBM = pl.BlockSpec(memory_space=pltpu.HBM)


def in_hbm(array):
    return pltpu.with_memory_space_constraint(array, pltpu.HBM)


def in_vmem(array):
    return pltpu.with_memory_space_constraint(array, pltpu.VMEM)


def turned(phase, total):
    bits = total.bit_length() - 1
    wrapped = phase & (total - 1)
    quarter = (wrapped + total // 8) >> (bits - 2)
    rest = wrapped - (quarter << (bits - 2))
    x = rest.astype(jnp.float32) * (2.0 * math.pi / total)
    y = x * x
    sine = x + x * y * (-1.6666654611e-1 + y * (8.3321608736e-3 - y * 1.9515295891e-4))
    cosine = (
        1.0
        - 0.5 * y
        + y * y * (4.166664568298827e-2 + y * (-1.388731625493765e-3 + y * 2.443315711809948e-5))
    )
    odd = (quarter & 1) == 1
    even_part = jnp.where(odd, sine, cosine)
    odd_part = jnp.where(odd, cosine, sine)
    flip = ((quarter + 1) & 2) == 2
    below = (quarter & 2) == 2
    return jnp.where(flip, -even_part, even_part), jnp.where(below, odd_part, -odd_part)


def as_column(scalars, rows, dtype):
    row = lax.broadcasted_iota(jnp.int32, (rows, LANES), 0)
    column = jnp.zeros((rows, LANES), dtype)
    for r in range(rows):
        column = jnp.where(row == r, scalars[r], column)
    return column


def transform_body(
    first_ref, start_ref, lines_ref, after_ref, v_ref, c_ref, out_ref,
    even_ref, odd_ref, raw_ref, cos_0, sin_0, cos_1, sin_1, turn_0, turn_1, v_in, c_in, sems,
    *, inner, total
):
    ports, times = v_ref.shape
    both = 2 * ports
    outer = times // inner
    half = inner // 2
    cols = lines_ref.shape[1] // 2

    def copies(s):
        at = pl.ds(s * inner, inner)
        return (
            pltpu.make_async_copy(v_ref.at[:, at], v_in.at[:, at], sems.at[0, s]),
            pltpu.make_async_copy(c_ref.at[:, at], c_in.at[:, at], sems.at[1, s]),
        )

    def build(lines, cos_ref, sin_ref, turn_ref):
        def steps(count):
            return lax.broadcasted_iota(jnp.int32, (count, cols), 0)

        fine = 16
        coarse = half // fine
        fine_cos, fine_sin = turned(lines * (2 * steps(fine) + 1), 2 * total)
        coarse_cos, coarse_sin = turned(lines * (steps(coarse) * (2 * fine)), 2 * total)
        middle = 2 * (first_ref[0] + steps(outer) * inner + half) - 1
        turn_ref[:outer], turn_ref[outer:] = turned(lines * middle, 2 * total)
        for u in range(coarse):
            cos_u, sin_u = coarse_cos[u : u + 1], coarse_sin[u : u + 1]
            at = slice(u * fine, (u + 1) * fine)
            cos_ref[at] = (cos_u * fine_cos - sin_u * fine_sin).astype(jnp.bfloat16)
            sin_ref[at] = (sin_u * fine_cos + cos_u * fine_sin).astype(jnp.bfloat16)

    def spectra(cos_ref, sin_ref, turn_ref, base):
        group = max(1, 512 // both)
        re = jnp.zeros((both, cols), jnp.float32)
        im = jnp.zeros((both, cols), jnp.float32)
        for g in range(0, outer, group):
            at = slice(g * both, (g + group) * both)
            part_re = jnp.dot(even_ref[at], cos_ref[...], preferred_element_type=jnp.float32)
            part_im = jnp.dot(odd_ref[at], sin_ref[...], preferred_element_type=jnp.float32)
            for s in range(group):
                re_s = part_re[s * both : (s + 1) * both]
                im_s = part_im[s * both : (s + 1) * both]
                cos_s = turn_ref[g + s : g + s + 1]
                sin_s = turn_ref[outer + g + s : outer + g + s + 1]
                re = re + (re_s * cos_s - im_s * sin_s)
                im = im + (re_s * sin_s + im_s * cos_s)
        for j in range(cols // LANES):
            at = slice(j * LANES, (j + 1) * LANES)
            out_ref[base + j, :both] = re[:, at]
            out_ref[base + j, both:] = im[:, at]

    @pl.when(pl.program_id(0) == 0)
    def _():
        for s in range(outer):
            for copy in copies(s):
                copy.start()
        build(lines_ref[:, :cols], cos_0, sin_0, turn_0)
        start = as_column(start_ref, ports, jnp.int32)[:, :1]
        row = lax.broadcasted_iota(jnp.int32, (FLIP, FLIP), 0)
        col = lax.broadcasted_iota(jnp.int32, (FLIP, FLIP), 1)
        flip = jnp.where(row + col == FLIP - 1, 1.0, 0.0).astype(jnp.bfloat16)
        group = max(1, 256 // both)
        for g in range(0, outer, group):
            for s in range(g, g + group):
                at = slice(s * inner, (s + 1) * inner)
                time = first_ref[0] + s * inner
                time = time + lax.broadcasted_iota(jnp.int32, (ports, inner), 1)
                keep = time >= start
                low = s * both
                for copy in copies(s):
                    copy.wait()
                raw_ref[low : low + ports] = jnp.where(keep, v_in[:, at], 0.0).astype(jnp.bfloat16)
                raw_ref[low + ports : low + both] = jnp.where(keep, c_in[:, at], 0.0).astype(
                    jnp.bfloat16
                )
            at = slice(g * both, (g + group) * both)
            for q in range(half // FLIP):
                to = slice(q * FLIP, (q + 1) * FLIP)
                behind = jnp.dot(
                    raw_ref[at, half - (q + 1) * FLIP : half - q * FLIP],
                    flip,
                    preferred_element_type=jnp.float32,
                )
                ahead = raw_ref[at, half + q * FLIP : half + (q + 1) * FLIP].astype(jnp.float32)
                even_ref[at, to] = (ahead + behind).astype(jnp.bfloat16)
                odd_ref[at, to] = (ahead - behind).astype(jnp.bfloat16)

    build(lines_ref[:, cols:], cos_1, sin_1, turn_1)
    spectra(cos_0, sin_0, turn_0, 0)
    build(after_ref[:, :cols], cos_0, sin_0, turn_0)
    spectra(cos_1, sin_1, turn_1, cols // LANES)


def transform(first, start, freq_index, voltages, currents, total):
    ports, times = voltages.shape
    both = 2 * ports
    count = freq_index.shape[0]
    outer = times // INNER
    half = INNER // 2
    steps = count // (2 * COLUMNS)
    table = pltpu.VMEM((half, COLUMNS), jnp.bfloat16)
    turn = pltpu.VMEM((2 * outer, COLUMNS), jnp.float32)
    lines = in_hbm(freq_index.reshape(1, count))
    return pl.pallas_call(
        functools.partial(transform_body, inner=INNER, total=total),
        grid=(steps,),
        in_specs=[
            SMEM,
            SMEM,
            pl.BlockSpec((1, 2 * COLUMNS), lambda i: (0, i)),
            pl.BlockSpec((1, 2 * COLUMNS), lambda i: (0, jnp.minimum(i + 1, steps - 1))),
            HBM,
            HBM,
        ],
        out_specs=pl.BlockSpec((2 * COLUMNS // LANES, 2 * both, LANES), lambda i: (i, 0, 0)),
        out_shape=pltpu.VMEM((count // LANES, 2 * both, LANES), jnp.float32),
        scratch_shapes=[
            pltpu.VMEM((outer * both, half), jnp.bfloat16),
            pltpu.VMEM((outer * both, half), jnp.bfloat16),
            pltpu.VMEM((outer * both, INNER), jnp.bfloat16),
            table,
            table,
            table,
            table,
            turn,
            turn,
            pltpu.VMEM((ports, times), jnp.float32),
            pltpu.VMEM((ports, times), jnp.float32),
            pltpu.SemaphoreType.DMA((2, outer)),
        ],
        compiler_params=pltpu.CompilerParams(
            dimension_semantics=("arbitrary",), vmem_limit_bytes=48 << 20
        ),
        name="spectrum",
    )(first.reshape(1), in_hbm(start), lines, lines, in_hbm(voltages), in_hbm(currents))


def waves_body(impedance_ref, parts_ref, sent_ref, own_ref, *, scale):
    ports = own_ref.shape[0]
    total = jnp.sum(parts_ref[...], axis=0) * scale
    z = as_column(impedance_ref, ports, jnp.float32)
    inverse = 1.0 / (2.0 * jnp.sqrt(z))
    for r in range(2):
        at = slice(r * LANES, (r + 1) * LANES)
        v = total[2 * r * ports : (2 * r + 1) * ports]
        c = total[(2 * r + 1) * ports : (2 * r + 2) * ports]
        a = (v + z * c) * inverse
        own_ref[:, at] = (v - z * c) * inverse
        for d in range(sent_ref.shape[0]):
            sent_ref[d, :, at] = a


def pick_body(pairing_ref, every_ref, own_ref, sent_ref, made_ref, q_ref):
    ports = own_ref.shape[0]
    for p in range(ports):
        q = pairing_ref[p]
        q_ref[p : p + 1] = every_ref[q // ports, pl.ds(q % ports, 1)]
    q_re, q_im = q_ref[:, :LANES], q_ref[:, LANES:]
    b_re, b_im = own_ref[:, :LANES], own_ref[:, LANES:]
    power = q_re * q_re + q_im * q_im
    made_ref[0] = b_re * q_re + b_im * q_im
    made_ref[1] = b_im * q_re - b_re * q_im
    made_ref[2] = power
    padded = jnp.concatenate([power, jnp.zeros((LANES - ports, LANES), jnp.float32)], axis=0)
    share = jnp.sum(padded.T, axis=0, keepdims=True)
    sent_ref[...] = jnp.broadcast_to(share, sent_ref.shape)


def divide_body(shares_ref, made_ref, out_ref, *, width):
    ports = out_ref.shape[1]
    summed = jnp.sum(shares_ref[...], axis=0, keepdims=True)
    mean = jnp.broadcast_to(summed / width + 1e-06, (LANES, LANES)).T[:ports]
    inverse = 1.0 / jnp.maximum(made_ref[2], 0.1 * mean)
    out_ref[0] = made_ref[0] * inverse
    out_ref[1] = made_ref[1] * inverse


def body(voltages, currents, impedance, freq_index, window_start, pairing):
    ports, times = voltages.shape
    width = freq_index.shape[0]
    times_count, ports_count = lax.axis_size("tm"), lax.axis_size("port")
    total = times * times_count
    first = lax.axis_index("tm") * times
    parts = transform(first, window_start, freq_index, voltages, currents, total)
    parts = lax.all_to_all(in_vmem(parts), "tm", 0, 0, tiled=True)
    sent, own = pl.pallas_call(
        functools.partial(waves_body, scale=1.0 / math.sqrt(total)),
        in_specs=[SMEM, VMEM],
        out_specs=[VMEM, VMEM],
        out_shape=[
            pltpu.VMEM((ports_count, ports, 2 * LANES), jnp.float32),
            pltpu.VMEM((ports, 2 * LANES), jnp.float32),
        ],
        name="waves",
    )(in_hbm(impedance), in_vmem(parts))
    every = lax.all_to_all(in_vmem(sent), "port", 0, 0, tiled=True)
    shares, made = pl.pallas_call(
        pick_body,
        in_specs=[SMEM, VMEM, VMEM],
        out_specs=[VMEM, VMEM],
        out_shape=[
            pltpu.VMEM((times_count, LANES), jnp.float32),
            pltpu.VMEM((3, ports, LANES), jnp.float32),
        ],
        scratch_shapes=[pltpu.VMEM((ports, 2 * LANES), jnp.float32)],
        name="pick",
    )(in_hbm(pairing), in_vmem(every), in_vmem(own))
    shares = lax.all_to_all(in_vmem(shares), "tm", 0, 0, tiled=True)
    return pl.pallas_call(
        functools.partial(divide_body, width=width),
        in_specs=[VMEM, VMEM],
        out_specs=VMEM,
        out_shape=jax.ShapeDtypeStruct((2, ports, LANES), jnp.float32),
        name="divide",
    )(in_vmem(shares), in_vmem(made))


def solution(mesh):
    placed = (P("port", "tm"), P("port", "tm"), P("port"), P(), P("port"), P("port"))
    return jax.shard_map(
        body, mesh=mesh, in_specs=placed, out_specs=P(None, "port", "tm"), check_vma=False
    )
```

time: 71 us -> 59.9 us (0.84)
  Pallas kernels: 17.3 us -> 12 us
  local copies, waits for them, and re-layouts: 4.53 us -> 0 us
  blocking collectives: 48.6 us -> 47.7 us
    unnamed x8 -> x0, local copies, waits for them, and re-layouts: 4.53 us -> none
    pallas_call x3, Pallas kernels: 15.3 us -> 11.3 us  [the longest x1 9.55 us: transform(): pl.pallas_call(functools.partial(transform_body, inner=INNER, total=total...]
    pallas_call x1, Pallas kernels: 2.01 us -> 0.73 us  [body(): pl.pallas_call(functools.partial(waves_body, scale=1.0 / math.sqrt(total)...]
    all_to_all x3, blocking collectives: 48.6 us -> 47.7 us  [the longest x1 24.8 us: body(): parts = lax.all_to_all(in_vmem(parts), 'tm', 0, 0, tiled=True)]
where the time goes in v3:
time: 59.9 us; the launch traced here: 59.7 us
  blocking collectives  47.7 us (80%)
  Pallas kernels  12 us (20%)
    all_to_all x1, blocking collectives, body(): parts = lax.all_to_all(in_vmem(parts), 'tm', 0, 0, tiled=True)  24.8 us
    all_to_all x1, blocking collectives, body(): every = lax.all_to_all(in_vmem(sent), 'port', 0, 0, tiled=True)  11.6 us
    all_to_all x1, blocking collectives, body(): shares = lax.all_to_all(in_vmem(shares), 'tm', 0, 0, tiled=True)  11.2 us
    pallas_call x1, Pallas kernels, transform(): pl.pallas_call(functools.partial(transform_body, inner=INNER, total=total...  9.55 us

profile of v3, /device:TPU:0, one launch (start us, length us, event | category | flops | bytes accessed | tf_op | source)
XLA Modules:
  0.0 59.7 jit_solution(7553606324312341445)
XLA Ops:
  0.0 9.6 %spectrum.1 = f32[16,128,128]{2,1,0:T(8,128)S(1)} custom-call(s32[1]{0:T(128)} %bitcast.first_ref, s32[32]{0:T(128)} %start_ref.1, s32[1,2048]{1,0:T(1,128)} %bitcast.8, s32[1,2048]{1,0:T(1,128)} %bitcast.9, f32[32,16384]{1,0:T(8,128)} %v_ref.1, f32[32,16384]{1,0:T(8,128)} %c_ref.1), custom_call_target="tpu_custom_call" | custom-call | tf_op jit(solution)/shard_map/spectrum/pallas_call | solution.py:163
  9.6 24.8 %all_to_all.21.parts_ref = f32[16,128,128]{2,1,0:T(8,128)S(1)} all-to-all(f32[16,128,128]{2,1,0:T(8,128)S(1)} %spectrum.1), channel_id=1, replica_groups=mesh['tm'=16,'port'=8] {'tm'}, dimensions={0} | all-to-all | bytes 2097152 | tf_op jit(solution)/shard_map/all_to_all | solution.py:244
  34.4 0.7 %waves.1 = (f32[8,32,256]{2,1,0:T(8,128)S(1)}, f32[32,256]{1,0:T(8,128)S(1)}) custom-call(f32[32]{0:T(128)} %impedance_ref.1, f32[16,128,128]{2,1,0:T(8,128)S(1)} %all_to_all.21.parts_ref), custom_call_target="tpu_custom_call" | custom-call | tf_op jit(solution)/shard_map/waves/pallas_call | solution.py:245
  35.1 11.6 %all_to_all.22.every_ref = f32[8,32,256]{2,1,0:T(8,128)S(1)} all-to-all(f32[8,32,256]{2,1,0:T(8,128)S(1)} %get-tuple-element.9), channel_id=1, replica_groups=mesh['tm'=16,'port'=8] {'port'}, dimensions={0} | all-to-all | bytes 524288 | tf_op jit(solution)/shard_map/all_to_all | solution.py:255
  46.7 1.0 %pick.1 = (f32[16,128]{1,0:T(8,128)S(1)}, f32[3,32,128]{2,1,0:T(8,128)S(1)}) custom-call(s32[32]{0:T(128)} %pairing_ref.1, f32[8,32,256]{2,1,0:T(8,128)S(1)} %all_to_all.22.every_ref, f32[32,256]{1,0:T(8,128)S(1)} %get-tuple-element.10.own_ref), custom_call_target="tpu_custom_call" | custom-call | tf_op jit(solution)/shard_map/pick/pallas_call | solution.py:256
  47.7 11.2 %all_to_all.23 = f32[16,1,128]{2,1,0:T(1,128)S(1)} all-to-all(f32[16,1,128]{2,1,0:T(1,128)S(1)} %bitcast.7), channel_id=1, replica_groups=mesh['tm'=16,'port'=8] {'tm'}, dimensions={0} | all-to-all | bytes 16384 | tf_op jit(solution)/shard_map/all_to_all | solution.py:267
  59.0 0.7 %divide.1 = f32[2,32,128]{2,1,0:T(8,128)} custom-call(f32[16,128]{1,0:T(8,128)S(1)} %bitcast.6, f32[3,32,128]{2,1,0:T(8,128)S(1)} %get-tuple-element.12.made_ref), custom_call_target="tpu_custom_call" | custom-call | tf_op jit(solution)/shard_map/divide/pallas_call | solution.py:268

commit v4 on v3

--- a/solution.py
+++ b/solution.py
@@ -7,6 +7,7 @@
 from jax.experimental import pallas as pl
 from jax.experimental.pallas import tpu as pltpu
 from jax.sharding import PartitionSpec as P
+
 
 LANES = 128
 COLUMNS = 256
@@ -194,84 +195,126 @@
     )(first.reshape(1), in_hbm(start), lines, lines, in_hbm(voltages), in_hbm(currents))
 
 
-def waves_body(impedance_ref, parts_ref, sent_ref, own_ref, *, scale):
+def waves_body(impedance_ref, parts_ref, sent_ref, own_ref, share_ref, *, scale):
     ports = own_ref.shape[0]
     total = jnp.sum(parts_ref[...], axis=0) * scale
     z = as_column(impedance_ref, ports, jnp.float32)
     inverse = 1.0 / (2.0 * jnp.sqrt(z))
+    power = jnp.zeros((ports, LANES), jnp.float32)
     for r in range(2):
         at = slice(r * LANES, (r + 1) * LANES)
         v = total[2 * r * ports : (2 * r + 1) * ports]
         c = total[(2 * r + 1) * ports : (2 * r + 2) * ports]
         a = (v + z * c) * inverse
+        power = power + a * a
+        sent_ref[:, at] = a
         own_ref[:, at] = (v - z * c) * inverse
-        for d in range(sent_ref.shape[0]):
-            sent_ref[d, :, at] = a
-
-
-def pick_body(pairing_ref, every_ref, own_ref, sent_ref, made_ref, q_ref):
+    padded = jnp.concatenate([power, jnp.zeros((LANES - ports, LANES), jnp.float32)], axis=0)
+    share = jnp.sum(padded.T, axis=0, keepdims=True)
+    share_ref[...] = jnp.broadcast_to(share, share_ref.shape)
+
+
+def means_body(shares_ref, out_ref, *, ports, width):
+    row = lax.broadcasted_iota(jnp.int32, shares_ref.shape, 0)
+    shares = shares_ref[...]
+    lane = lax.broadcasted_iota(jnp.int32, (1, LANES), 1)
+    sums = [
+        jnp.sum(jnp.where((row & 1) == c, shares, 0.0), axis=0, keepdims=True) for c in range(2)
+    ]
+    both = jnp.where(lane < ports, sums[0], pltpu.roll(sums[1], ports, 1))
+    out_ref[...] = jnp.broadcast_to(both / width + 1e-06, out_ref.shape)
+
+
+def scatter_body(
+    place_ref, pairing_ref, same_ref, other_ref, mean_0, mean_1, mean_2, mean_3,
+    own_ref, out_ref, every_ref, table_ref, q_ref, mean_ref,
+):
     ports = own_ref.shape[0]
+    means = (mean_0, mean_1, mean_2, mean_3)
+    place = place_ref[0]
+    chips = len(means)
+    every_ref[0] = same_ref[...]
+    every_ref[1] = other_ref[...]
+    lane = lax.broadcasted_iota(jnp.int32, (1, LANES), 1)
+    for k in range(0, chips, 2):
+        row = jnp.where(lane < 2 * ports, means[k][:1], pltpu.roll(means[k + 1][:1], 2 * ports, 1))
+        table_ref[k * 2 * ports : (k + 2) * 2 * ports] = jnp.broadcast_to(row, (LANES, LANES)).T
     for p in range(ports):
         q = pairing_ref[p]
-        q_ref[p : p + 1] = every_ref[q // ports, pl.ds(q % ports, 1)]
+        holder = q // ports
+        back = (place // 2 - holder // 2) & (chips - 1)
+        rest = q % ports
+        q_ref[p : p + 1] = every_ref[(place ^ holder) & 1, back, pl.ds(rest, 1)]
+        mean_ref[p : p + 1] = table_ref[pl.ds((2 * back + (holder & 1)) * ports + rest, 1)]
     q_re, q_im = q_ref[:, :LANES], q_ref[:, LANES:]
     b_re, b_im = own_ref[:, :LANES], own_ref[:, LANES:]
     power = q_re * q_re + q_im * q_im
-    made_ref[0] = b_re * q_re + b_im * q_im
-    made_ref[1] = b_im * q_re - b_re * q_im
-    made_ref[2] = power
-    padded = jnp.concatenate([power, jnp.zeros((LANES - ports, LANES), jnp.float32)], axis=0)
-    share = jnp.sum(padded.T, axis=0, keepdims=True)
-    sent_ref[...] = jnp.broadcast_to(share, sent_ref.shape)
-
-
-def divide_body(shares_ref, made_ref, out_ref, *, width):
-    ports = out_ref.shape[1]
-    summed = jnp.sum(shares_ref[...], axis=0, keepdims=True)
-    mean = jnp.broadcast_to(summed / width + 1e-06, (LANES, LANES)).T[:ports]
-    inverse = 1.0 / jnp.maximum(made_ref[2], 0.1 * mean)
-    out_ref[0] = made_ref[0] * inverse
-    out_ref[1] = made_ref[1] * inverse
+    inverse = 1.0 / jnp.maximum(power, 0.1 * mean_ref[...])
+    out_ref[0] = (b_re * q_re + b_im * q_im) * inverse
+    out_ref[1] = (b_im * q_re - b_re * q_im) * inverse
 
 
 def body(voltages, currents, impedance, freq_index, window_start, pairing):
     ports, times = voltages.shape
     width = freq_index.shape[0]
     times_count, ports_count = lax.axis_size("tm"), lax.axis_size("port")
+    chips = ports_count // 2
     total = times * times_count
     first = lax.axis_index("tm") * times
     parts = transform(first, window_start, freq_index, voltages, currents, total)
     parts = lax.all_to_all(in_vmem(parts), "tm", 0, 0, tiled=True)
-    sent, own = pl.pallas_call(
+    sent, own, share = pl.pallas_call(
         functools.partial(waves_body, scale=1.0 / math.sqrt(total)),
         in_specs=[SMEM, VMEM],
-        out_specs=[VMEM, VMEM],
+        out_specs=[VMEM, VMEM, VMEM],
         out_shape=[
-            pltpu.VMEM((ports_count, ports, 2 * LANES), jnp.float32),
             pltpu.VMEM((ports, 2 * LANES), jnp.float32),
+            pltpu.VMEM((ports, 2 * LANES), jnp.float32),
+            pltpu.VMEM((2 * times_count, LANES), jnp.float32),
         ],
         name="waves",
     )(in_hbm(impedance), in_vmem(parts))
-    every = lax.all_to_all(in_vmem(sent), "port", 0, 0, tiled=True)
-    shares, made = pl.pallas_call(
-        pick_body,
-        in_specs=[SMEM, VMEM, VMEM],
-        out_specs=[VMEM, VMEM],
-        out_shape=[
-            pltpu.VMEM((times_count, LANES), jnp.float32),
-            pltpu.VMEM((3, ports, LANES), jnp.float32),
-        ],
-        scratch_shapes=[pltpu.VMEM((ports, 2 * LANES), jnp.float32)],
-        name="pick",
-    )(in_hbm(pairing), in_vmem(every), in_vmem(own))
-    shares = lax.all_to_all(in_vmem(shares), "tm", 0, 0, tiled=True)
+    columns = [
+        [ports_count * t + 2 * x + c for t in range(times_count) for c in range(2)]
+        for x in range(chips)
+    ]
+    ahead = [
+        [(i, (i + 2 * k) % ports_count) for i in range(ports_count)] for k in range(1, chips)
+    ]
+    shares = lax.all_to_all(
+        in_vmem(share), ("tm", "port"), 0, 0, tiled=True, axis_index_groups=columns
+    )
+    along = [sent]
+    for k in range(1, chips):
+        along.append(lax.ppermute(sent, "port", ahead[k - 1]))
+    same = jnp.stack(along)
+    other = lax.ppermute(same, "port", [(i, i ^ 1) for i in range(ports_count)])
+    mean = pl.pallas_call(
+        functools.partial(means_body, ports=ports, width=width),
+        in_specs=[VMEM],
+        out_specs=VMEM,
+        out_shape=pltpu.VMEM((8, LANES), jnp.float32),
+        name="means",
+    )(in_vmem(shares))
+    means = [mean]
+    for k in range(1, chips):
+        means.append(lax.ppermute(mean, "port", ahead[k - 1]))
     return pl.pallas_call(
-        functools.partial(divide_body, width=width),
-        in_specs=[VMEM, VMEM],
+        scatter_body,
+        in_specs=[SMEM, SMEM] + [VMEM] * (chips + 3),
         out_specs=VMEM,
         out_shape=jax.ShapeDtypeStruct((2, ports, LANES), jnp.float32),
-        name="divide",
-    )(in_vmem(shares), in_vmem(made))
+        scratch_shapes=[
+            pltpu.VMEM((2, chips, ports, 2 * LANES), jnp.float32),
+            pltpu.VMEM((ports_count * ports, LANES), jnp.float32),
+            pltpu.VMEM((ports, 2 * LANES), jnp.float32),
+            pltpu.VMEM((ports, LANES), jnp.float32),
+        ],
+        name="scatter",
+    )(
+        lax.axis_index("port").reshape(1), in_hbm(pairing), in_vmem(same), in_vmem(other),
+        *map(in_vmem, means), in_vmem(own),
+    )
 
 
 def solution(mesh):

time: 59.9 us -> 64.2 us (1.072)
  blocking collectives: 47.7 us -> 36.2 us
  waiting for transfers between devices: 0 us -> 7.88 us
  starting transfers between devices: 0 us -> 7.53 us
    all_to_all x2 -> x1, blocking collectives: 22.8 us -> 11.4 us  [body(): lax.all_to_all(in_vmem(share), ('tm', 'port'), 0, 0, tiled=True, axis_ind...]
    ppermute x0 -> x7, waiting for transfers between devices: none -> 7.88 us  [the longest x3 4.25 us: body(): along.append(lax.ppermute(sent, 'port', ahead[k - 1]))]
    ppermute x0 -> x7, starting transfers between devices: none -> 7.53 us  [the longest x3 4.52 us: body(): along.append(lax.ppermute(sent, 'port', ahead[k - 1]))]
  transfers between devices with their start and end apart: 0 -> 7, of which waited for: 0 -> 5; matrix products, arithmetic and copies ran while one was open for 0% -> 0% of each run, Pallas kernels for 0% -> 0%
where the time goes in v4:
time: 64.2 us; the launch traced here: 64 us
  blocking collectives  36.2 us (56%)
  Pallas kernels  12.3 us (19%)
  waiting for transfers between devices  7.88 us (12%)
  starting transfers between devices  7.53 us (12%)
    all_to_all x1, blocking collectives, body(): parts = lax.all_to_all(in_vmem(parts), 'tm', 0, 0, tiled=True)  24.8 us
    all_to_all x1, blocking collectives, body(): lax.all_to_all(in_vmem(share), ('tm', 'port'), 0, 0, tiled=True, axis_ind...  11.4 us
    pallas_call x1, Pallas kernels, transform(): pl.pallas_call(functools.partial(transform_body, inner=INNER, total=total...  9.55 us
    ppermute x3, starting transfers between devices, body(): along.append(lax.ppermute(sent, 'port', ahead[k - 1]))  4.52 us
    ppermute x3, waiting for transfers between devices, body(): along.append(lax.ppermute(sent, 'port', ahead[k - 1]))  4.25 us
    ppermute x3, waiting for transfers between devices, body(): means.append(lax.ppermute(mean, 'port', ahead[k - 1]))  3.63 us
    ppermute x3, starting transfers between devices, body(): means.append(lax.ppermute(mean, 'port', ahead[k - 1]))  2.92 us
    pallas_call x1, Pallas kernels, body(): pl.pallas_call(scatter_body, in_specs=[SMEM, SMEM] + [VMEM] * (chips + 3)...  1.84 us
  transfers between devices with their start and end apart: 7, of which 5 were waited for; matrix products, arithmetic and copies ran while one was open for 0% of the time, Pallas kernels for 0%

profile of v4, /device:TPU:0, one launch (start us, length us, event | category | flops | bytes accessed | tf_op | source)
XLA Modules:
  0.0 64.0 jit_solution(1030125887408295979)
XLA Ops:
  0.0 9.6 %spectrum.1 = f32[16,128,128]{2,1,0:T(8,128)S(1)} custom-call(s32[1]{0:T(128)} %bitcast.1.first_ref, s32[32]{0:T(128)} %start_ref.1, s32[1,2048]{1,0:T(1,128)} %bitcast.14, s32[1,2048]{1,0:T(1,128)} %bitcast.15, f32[32,16384]{1,0:T(8,128)} %v_ref.1, f32[32,16384]{1,0:T(8,128)} %c_ref.1), custom_call_target="tpu_custom_call" | custom-call | tf_op jit(solution)/shard_map/spectrum/pallas_call | solution.py:164
  9.6 24.8 %all_to_all.16.parts_ref = f32[16,128,128]{2,1,0:T(8,128)S(1)} all-to-all(f32[16,128,128]{2,1,0:T(8,128)S(1)} %spectrum.1), channel_id=1, replica_groups=mesh['tm'=16,'port'=8] {'tm'}, dimensions={0} | all-to-all | bytes 2097152 | tf_op jit(solution)/shard_map/all_to_all | solution.py:265
  34.4 0.9 %waves.1 = (f32[32,256]{1,0:T(8,128)S(1)}, f32[32,256]{1,0:T(8,128)S(1)}, f32[32,128]{1,0:T(8,128)S(1)}) custom-call(f32[32]{0:T(128)} %impedance_ref.1, f32[16,128,128]{2,1,0:T(8,128)S(1)} %all_to_all.16.parts_ref), custom_call_target="tpu_custom_call" | custom-call | tf_op jit(solution)/shard_map/waves/pallas_call | solution.py:266
  35.2 2.8 %collective-permute-start.2 = (f32[32,256]{1,0:T(8,128)S(1)}, f32[32,256]{1,0:T(8,128)S(1)}, u32[]{:S(2)}, u32[]{:S(2)}) collective-permute-start(f32[32,256]{1,0:T(8,128)S(1)} %get-tuple-element.8), channel_id=1, source_target_pairs={{0,6},{1,7},{2,0},{3,1},{4,2},{5,3},{6,4},{7,5},{8,14},{9,15},{10,... | collective-permute-start | bytes 98312 | tf_op jit(solution)/shard_map/ppermute | solution.py:289
  38.0 0.8 %collective-permute-start.1 = (f32[32,256]{1,0:T(8,128)S(1)}, f32[32,256]{1,0:T(8,128)S(1)}, u32[]{:S(2)}, u32[]{:S(2)}) collective-permute-start(f32[32,256]{1,0:T(8,128)S(1)} %get-tuple-element.8), channel_id=1, source_target_pairs={{0,4},{1,5},{2,6},{3,7},{4,0},{5,1},{6,2},{7,3},{8,12},{9,13},{10,... | collective-permute-start | bytes 98312 | tf_op jit(solution)/shard_map/ppermute | solution.py:289
  38.9 0.9 %collective-permute-start = (f32[32,256]{1,0:T(8,128)S(1)}, f32[32,256]{1,0:T(8,128)S(1)}, u32[]{:S(2)}, u32[]{:S(2)}) collective-permute-start(f32[32,256]{1,0:T(8,128)S(1)} %get-tuple-element.8), channel_id=1, source_target_pairs={{0,2},{1,3},{2,4},{3,5},{4,6},{5,7},{6,0},{7,1},{8,10},{9,11},{10,... | collective-permute-start | bytes 98312 | tf_op jit(solution)/shard_map/ppermute | solution.py:289
  39.7 0.0 collective-permute-done.2
  39.7 3.7 %collective-permute-done.1 = f32[32,256]{1,0:T(8,128)S(1)} collective-permute-done((f32[32,256]{1,0:T(8,128)S(1)}, f32[32,256]{1,0:T(8,128)S(1)}, u32[]{:S(2)}, u32[]{:S(2)}) %collective-permute-start.1) | collective-permute-done | bytes 32800 | tf_op jit(solution)/shard_map/ppermute | solution.py:289
  43.5 0.5 collective-permute-done
  44.0 0.1 collective-permute-start.3
  44.1 11.4 %all_to_all.17 = f32[32,1,128]{2,1,0:T(1,128)S(1)} all-to-all(f32[32,1,128]{2,1,0:T(1,128)S(1)} %bitcast.13), channel_id=1, replica_groups={{0,1,8,9,16,17,24,25,32,33,40,41,48,49,56,57,64,65,72,73,80,81,88,89,96..., dimensions={0} | all-to-all | bytes 32768 | tf_op jit(solution)/shard_map/all_to_all | solution.py:284
  55.5 0.1 means.1.mean_0
  55.6 0.4 collective-permute-start.6
  56.0 1.3 %collective-permute-start.5 = (f32[8,128]{1,0:T(8,128)S(1)}, f32[8,128]{1,0:T(8,128)S(1)}, u32[]{:S(2)}, u32[]{:S(2)}) collective-permute-start(f32[8,128]{1,0:T(8,128)S(1)} %means.1.mean_0), channel_id=1, source_target_pairs={{0,4},{1,5},{2,6},{3,7},{4,0},{5,1},{6,2},{7,3},{8,12},{9,13},{10,... | collective-permute-start | bytes 12296 | tf_op jit(solution)/shard_map/ppermute | solution.py:301
  57.3 1.2 %collective-permute-start.4 = (f32[8,128]{1,0:T(8,128)S(1)}, f32[8,128]{1,0:T(8,128)S(1)}, u32[]{:S(2)}, u32[]{:S(2)}) collective-permute-start(f32[8,128]{1,0:T(8,128)S(1)} %means.1.mean_0), channel_id=1, source_target_pairs={{0,2},{1,3},{2,4},{3,5},{4,6},{5,7},{6,0},{7,1},{8,10},{9,11},{10,... | collective-permute-start | bytes 12296 | tf_op jit(solution)/shard_map/ppermute | solution.py:301
  58.5 0.7 %collective-permute-done.6.mean_3 = f32[8,128]{1,0:T(8,128)S(1)} collective-permute-done((f32[8,128]{1,0:T(8,128)S(1)}, f32[8,128]{1,0:T(8,128)S(1)}, u32[]{:S(2)}, u32[]{:S(2)}) %collective-permute-start.6) | collective-permute-done | bytes 4128 | tf_op jit(solution)/shard_map/ppermute | solution.py:301
  59.2 1.9 %collective-permute-done.5.mean_2 = f32[8,128]{1,0:T(8,128)S(1)} collective-permute-done((f32[8,128]{1,0:T(8,128)S(1)}, f32[8,128]{1,0:T(8,128)S(1)}, u32[]{:S(2)}, u32[]{:S(2)}) %collective-permute-start.5) | collective-permute-done | bytes 4128 | tf_op jit(solution)/shard_map/ppermute | solution.py:301
  61.1 1.1 %collective-permute-done.4.mean_1 = f32[8,128]{1,0:T(8,128)S(1)} collective-permute-done((f32[8,128]{1,0:T(8,128)S(1)}, f32[8,128]{1,0:T(8,128)S(1)}, u32[]{:S(2)}, u32[]{:S(2)}) %collective-permute-start.4) | collective-permute-done | bytes 4128 | tf_op jit(solution)/shard_map/ppermute | solution.py:301
  62.2 0.0 collective-permute-done.3.other_ref
  62.2 1.8 %scatter.1 = f32[2,32,128]{2,1,0:T(8,128)} custom-call(s32[1]{0:T(128)} %bitcast.place_ref, s32[32]{0:T(128)} %pairing_ref.1, f32[4,32,256]{2,1,0:T(8,128)S(1)} %pad_maximum_fusion.same_ref, f32[4,32,256]{2,1,0:T(8,128)S(1)} %collective-permute-done.3.other_ref, f32[8,128]{1,0:T(8,128)S(1)} %means.1.mean_0, f32[8,128]{1,0:T(8,128)S(1)} %collective-permute-done.4.mean_1, ...), custom_call_target="tpu_custom_call" | custom-call | tf_op jit(solution)/shard_map/scatter/pallas_call | solution.py:302
  (1 shorter events, 0.0 us)
Async XLA Ops:
  35.2 4.5 %collective-permute-start.2 = (f32[32,256]{1,0:T(8,128)S(1)}, f32[32,256]{1,0:T(8,128)S(1)}, u32[]{:S(2)}, u32[]{:S(2)}) collective-permute-start(f32[32,256]{1,0:T(8,128)S(1)} %get-tuple-element.8), channel_id=1, source_target_pairs={{0,6},{1,7},{2,0},{3,1},{4,2},{5,3},{6,4},{7,5},{8,14},{9,15},{10,... | collective-permute-start | bytes 98312 | tf_op jit(solution)/shard_map/ppermute | solution.py:289
  38.0 5.4 %collective-permute-start.1 = (f32[32,256]{1,0:T(8,128)S(1)}, f32[32,256]{1,0:T(8,128)S(1)}, u32[]{:S(2)}, u32[]{:S(2)}) collective-permute-start(f32[32,256]{1,0:T(8,128)S(1)} %get-tuple-element.8), channel_id=1, source_target_pairs={{0,4},{1,5},{2,6},{3,7},{4,0},{5,1},{6,2},{7,3},{8,12},{9,13},{10,... | collective-permute-start | bytes 98312 | tf_op jit(solution)/shard_map/ppermute | solution.py:289
  38.9 5.1 %collective-permute-start = (f32[32,256]{1,0:T(8,128)S(1)}, f32[32,256]{1,0:T(8,128)S(1)}, u32[]{:S(2)}, u32[]{:S(2)}) collective-permute-start(f32[32,256]{1,0:T(8,128)S(1)} %get-tuple-element.8), channel_id=1, source_target_pairs={{0,2},{1,3},{2,4},{3,5},{4,6},{5,7},{6,0},{7,1},{8,10},{9,11},{10,... | collective-permute-start | bytes 98312 | tf_op jit(solution)/shard_map/ppermute | solution.py:289
  44.0 18.2 %collective-permute-start.3 = (f32[4,32,256]{2,1,0:T(8,128)S(1)}, f32[4,32,256]{2,1,0:T(8,128)S(1)}, u32[]{:S(2)}, u32[]{:S(2)}) collective-permute-start(f32[4,32,256]{2,1,0:T(8,128)S(1)} %pad_maximum_fusion.same_ref), channel_id=1, source_target_pairs={{0,1},{1,0},{2,3},{3,2},{4,5},{5,4},{6,7},{7,6},{8,9},{9,8},{10,11... | collective-permute-start | bytes 393224 | tf_op jit(solution)/shard_map/ppermute | solution.py:291
  55.6 3.6 %collective-permute-start.6 = (f32[8,128]{1,0:T(8,128)S(1)}, f32[8,128]{1,0:T(8,128)S(1)}, u32[]{:S(2)}, u32[]{:S(2)}) collective-permute-start(f32[8,128]{1,0:T(8,128)S(1)} %means.1.mean_0), channel_id=1, source_target_pairs={{0,6},{1,7},{2,0},{3,1},{4,2},{5,3},{6,4},{7,5},{8,14},{9,15},{10,... | collective-permute-start | bytes 12296 | tf_op jit(solution)/shard_map/ppermute | solution.py:301
  56.0 5.1 %collective-permute-start.5 = (f32[8,128]{1,0:T(8,128)S(1)}, f32[8,128]{1,0:T(8,128)S(1)}, u32[]{:S(2)}, u32[]{:S(2)}) collective-permute-start(f32[8,128]{1,0:T(8,128)S(1)} %means.1.mean_0), channel_id=1, source_target_pairs={{0,4},{1,5},{2,6},{3,7},{4,0},{5,1},{6,2},{7,3},{8,12},{9,13},{10,... | collective-permute-start | bytes 12296 | tf_op jit(solution)/shard_map/ppermute | solution.py:301
  57.3 4.8 %collective-permute-start.4 = (f32[8,128]{1,0:T(8,128)S(1)}, f32[8,128]{1,0:T(8,128)S(1)}, u32[]{:S(2)}, u32[]{:S(2)}) collective-permute-start(f32[8,128]{1,0:T(8,128)S(1)} %means.1.mean_0), channel_id=1, source_target_pairs={{0,2},{1,3},{2,4},{3,5},{4,6},{5,7},{6,0},{7,1},{8,10},{9,11},{10,... | collective-permute-start | bytes 12296 | tf_op jit(solution)/shard_map/ppermute | solution.py:301

commit v5 on v4

--- a/solution.py
+++ b/solution.py
@@ -13,7 +13,6 @@
 COLUMNS = 256
 INNER = 1024
 FLIP = 256
-SMEM = pl.BlockSpec(memory_space=pltpu.SMEM)
 VMEM = pl.BlockSpec(memory_space=pltpu.VMEM)
 HBM = pl.BlockSpec(memory_space=pltpu.HBM)
 
@@ -56,15 +55,33 @@
 
 
 def transform_body(
-    first_ref, start_ref, lines_ref, after_ref, v_ref, c_ref, out_ref,
-    even_ref, odd_ref, raw_ref, cos_0, sin_0, cos_1, sin_1, turn_0, turn_1, v_in, c_in, sems,
+    start_ref, impedance_ref, pairing_ref, lines_ref, v_ref, c_ref, out_ref, z_ref, driven_ref,
+    even_ref, odd_ref, raw_ref, cos_0, sin_0, cos_1, sin_1, turn_0, turn_1, v_in, c_in, lines_in,
+    start_in, impedance_in, pairing_in, sems, small_sems,
     *, inner, total
 ):
     ports, times = v_ref.shape
     both = 2 * ports
     outer = times // inner
     half = inner // 2
-    cols = lines_ref.shape[1] // 2
+    cols = COLUMNS
+    first = lax.axis_index("tm") * times
+    step, steps_count = pl.program_id(0), pl.num_programs(0)
+
+    def lines_of(tile):
+        return lines_in[:, pl.ds(pl.multiple_of(tile * cols, cols), cols)]
+
+    small = [
+        pltpu.make_async_copy(a, b, small_sems.at[n])
+        for n, (a, b) in enumerate(
+            (
+                (lines_ref, lines_in),
+                (start_ref, start_in),
+                (impedance_ref, impedance_in),
+                (pairing_ref, pairing_in),
+            )
+        )
+    ]
 
     def copies(s):
         at = pl.ds(s * inner, inner)
@@ -81,7 +98,7 @@
         coarse = half // fine
         fine_cos, fine_sin = turned(lines * (2 * steps(fine) + 1), 2 * total)
         coarse_cos, coarse_sin = turned(lines * (steps(coarse) * (2 * fine)), 2 * total)
-        middle = 2 * (first_ref[0] + steps(outer) * inner + half) - 1
+        middle = 2 * (first + steps(outer) * inner + half) - 1
         turn_ref[:outer], turn_ref[outer:] = turned(lines * middle, 2 * total)
         for u in range(coarse):
             cos_u, sin_u = coarse_cos[u : u + 1], coarse_sin[u : u + 1]
@@ -109,13 +126,21 @@
             out_ref[base + j, :both] = re[:, at]
             out_ref[base + j, both:] = im[:, at]
 
-    @pl.when(pl.program_id(0) == 0)
+    @pl.when(step == 0)
     def _():
+        small[0].start()
         for s in range(outer):
             for copy in copies(s):
                 copy.start()
-        build(lines_ref[:, :cols], cos_0, sin_0, turn_0)
-        start = as_column(start_ref, ports, jnp.int32)[:, :1]
+        for copy in small[1:]:
+            copy.start()
+        small[0].wait()
+        build(lines_of(0), cos_0, sin_0, turn_0)
+        for copy in small[1:]:
+            copy.wait()
+        start = as_column(start_in, ports, jnp.int32)[:, :1]
+        z_ref[...] = as_column(impedance_in, ports, jnp.float32)
+        driven_ref[...] = as_column(pairing_in, ports, jnp.int32)
         row = lax.broadcasted_iota(jnp.int32, (FLIP, FLIP), 0)
         col = lax.broadcasted_iota(jnp.int32, (FLIP, FLIP), 1)
         flip = jnp.where(row + col == FLIP - 1, 1.0, 0.0).astype(jnp.bfloat16)
@@ -123,7 +148,7 @@
         for g in range(0, outer, group):
             for s in range(g, g + group):
                 at = slice(s * inner, (s + 1) * inner)
-                time = first_ref[0] + s * inner
+                time = first + s * inner
                 time = time + lax.broadcasted_iota(jnp.int32, (ports, inner), 1)
                 keep = time >= start
                 low = s * both
@@ -145,35 +170,35 @@
                 even_ref[at, to] = (ahead + behind).astype(jnp.bfloat16)
                 odd_ref[at, to] = (ahead - behind).astype(jnp.bfloat16)
 
-    build(lines_ref[:, cols:], cos_1, sin_1, turn_1)
+    build(lines_of(2 * step + 1), cos_1, sin_1, turn_1)
     spectra(cos_0, sin_0, turn_0, 0)
-    build(after_ref[:, :cols], cos_0, sin_0, turn_0)
+    build(lines_of(2 * jnp.minimum(step + 1, steps_count - 1)), cos_0, sin_0, turn_0)
     spectra(cos_1, sin_1, turn_1, cols // LANES)
 
 
-def transform(first, start, freq_index, voltages, currents, total):
+def transform(start, impedance, pairing, freq_index, voltages, currents, total):
     ports, times = voltages.shape
     both = 2 * ports
     count = freq_index.shape[0]
     outer = times // INNER
     half = INNER // 2
-    steps = count // (2 * COLUMNS)
     table = pltpu.VMEM((half, COLUMNS), jnp.bfloat16)
     turn = pltpu.VMEM((2 * outer, COLUMNS), jnp.float32)
-    lines = in_hbm(freq_index.reshape(1, count))
+    column = pl.BlockSpec((ports, LANES), lambda i: (0, 0))
     return pl.pallas_call(
         functools.partial(transform_body, inner=INNER, total=total),
-        grid=(steps,),
-        in_specs=[
-            SMEM,
-            SMEM,
-            pl.BlockSpec((1, 2 * COLUMNS), lambda i: (0, i)),
-            pl.BlockSpec((1, 2 * COLUMNS), lambda i: (0, jnp.minimum(i + 1, steps - 1))),
-            HBM,
-            HBM,
+        grid=(count // (2 * COLUMNS),),
+        in_specs=[HBM] * 6,
+        out_specs=[
+            pl.BlockSpec((2 * COLUMNS // LANES, 2 * both, LANES), lambda i: (i, 0, 0)),
+            column,
+            column,
         ],
-        out_specs=pl.BlockSpec((2 * COLUMNS // LANES, 2 * both, LANES), lambda i: (i, 0, 0)),
-        out_shape=pltpu.VMEM((count // LANES, 2 * both, LANES), jnp.float32),
+        out_shape=[
+            pltpu.VMEM((count // LANES, 2 * both, LANES), jnp.float32),
+            pltpu.VMEM((ports, LANES), jnp.float32),
+            pltpu.VMEM((ports, LANES), jnp.int32),
+        ],
         scratch_shapes=[
             pltpu.VMEM((outer * both, half), jnp.bfloat16),
             pltpu.VMEM((outer * both, half), jnp.bfloat16),
@@ -186,19 +211,27 @@
             turn,
             pltpu.VMEM((ports, times), jnp.float32),
             pltpu.VMEM((ports, times), jnp.float32),
+            pltpu.VMEM((1, count), jnp.int32),
+            pltpu.SMEM((ports,), jnp.int32),
+            pltpu.SMEM((ports,), jnp.float32),
+            pltpu.SMEM((ports,), jnp.int32),
             pltpu.SemaphoreType.DMA((2, outer)),
+            pltpu.SemaphoreType.DMA((4,)),
         ],
         compiler_params=pltpu.CompilerParams(
             dimension_semantics=("arbitrary",), vmem_limit_bytes=48 << 20
         ),
         name="spectrum",
-    )(first.reshape(1), in_hbm(start), lines, lines, in_hbm(voltages), in_hbm(currents))
-
-
-def waves_body(impedance_ref, parts_ref, sent_ref, own_ref, share_ref, *, scale):
+    )(
+        in_hbm(start), in_hbm(impedance), in_hbm(pairing), in_hbm(freq_index.reshape(1, count)),
+        in_hbm(voltages), in_hbm(currents),
+    )
+
+
+def waves_body(z_ref, parts_ref, sent_ref, own_ref, share_ref, *, scale):
     ports = own_ref.shape[0]
     total = jnp.sum(parts_ref[...], axis=0) * scale
-    z = as_column(impedance_ref, ports, jnp.float32)
+    z = z_ref[...]
     inverse = 1.0 / (2.0 * jnp.sqrt(z))
     power = jnp.zeros((ports, LANES), jnp.float32)
     for r in range(2):
@@ -225,31 +258,36 @@
     out_ref[...] = jnp.broadcast_to(both / width + 1e-06, out_ref.shape)
 
 
-def scatter_body(
-    place_ref, pairing_ref, same_ref, other_ref, mean_0, mean_1, mean_2, mean_3,
-    own_ref, out_ref, every_ref, table_ref, q_ref, mean_ref,
-):
+def scatter_body(driven_ref, same_ref, other_ref, mean_0, mean_1, mean_2, mean_3, own_ref, out_ref):
     ports = own_ref.shape[0]
     means = (mean_0, mean_1, mean_2, mean_3)
-    place = place_ref[0]
     chips = len(means)
-    every_ref[0] = same_ref[...]
-    every_ref[1] = other_ref[...]
-    lane = lax.broadcasted_iota(jnp.int32, (1, LANES), 1)
-    for k in range(0, chips, 2):
-        row = jnp.where(lane < 2 * ports, means[k][:1], pltpu.roll(means[k + 1][:1], 2 * ports, 1))
-        table_ref[k * 2 * ports : (k + 2) * 2 * ports] = jnp.broadcast_to(row, (LANES, LANES)).T
-    for p in range(ports):
-        q = pairing_ref[p]
-        holder = q // ports
-        back = (place // 2 - holder // 2) & (chips - 1)
-        rest = q % ports
-        q_ref[p : p + 1] = every_ref[(place ^ holder) & 1, back, pl.ds(rest, 1)]
-        mean_ref[p : p + 1] = table_ref[pl.ds((2 * back + (holder & 1)) * ports + rest, 1)]
-    q_re, q_im = q_ref[:, :LANES], q_ref[:, LANES:]
+    place = lax.axis_index("port")
+    driven = driven_ref[...]
+    holder = driven // ports
+    rest = driven % ports
+    back = (place // 2 - holder // 2) & (chips - 1)
+    core = holder & 1
+    lane = lax.broadcasted_iota(jnp.int32, (ports, LANES), 1)
+    spot = back * ports + rest
+    q = jnp.zeros((ports, 2 * LANES), jnp.float32)
+    for swapped, held_ref in enumerate((same_ref, other_ref)):
+        here = (lane == spot) & (((place + core) & 1) == swapped)
+        picks = jnp.where(here, 1.0, 0.0).astype(jnp.bfloat16)
+        left = held_ref[...].reshape(chips * ports, 2 * LANES)
+        for _ in range(3):
+            term = left.astype(jnp.bfloat16)
+            q = q + jnp.dot(picks, term, preferred_element_type=jnp.float32)
+            left = left - term.astype(jnp.float32)
+    level = jnp.zeros((ports, LANES), jnp.float32)
+    for k in range(chips):
+        here = (lane == core * ports + rest) & (back == k)
+        level = level + jnp.where(here, means[k][:1], 0.0)
+    mean = jnp.sum(level, axis=1, keepdims=True)
+    q_re, q_im = q[:, :LANES], q[:, LANES:]
     b_re, b_im = own_ref[:, :LANES], own_ref[:, LANES:]
     power = q_re * q_re + q_im * q_im
-    inverse = 1.0 / jnp.maximum(power, 0.1 * mean_ref[...])
+    inverse = 1.0 / jnp.maximum(power, 0.1 * mean)
     out_ref[0] = (b_re * q_re + b_im * q_im) * inverse
     out_ref[1] = (b_im * q_re - b_re * q_im) * inverse
 
@@ -260,12 +298,13 @@
     times_count, ports_count = lax.axis_size("tm"), lax.axis_size("port")
     chips = ports_count // 2
     total = times * times_count
-    first = lax.axis_index("tm") * times
-    parts = transform(first, window_start, freq_index, voltages, currents, total)
+    parts, z, driven = transform(
+        window_start, impedance, pairing, freq_index, voltages, currents, total
+    )
     parts = lax.all_to_all(in_vmem(parts), "tm", 0, 0, tiled=True)
     sent, own, share = pl.pallas_call(
         functools.partial(waves_body, scale=1.0 / math.sqrt(total)),
-        in_specs=[SMEM, VMEM],
+        in_specs=[VMEM, VMEM],
         out_specs=[VMEM, VMEM, VMEM],
         out_shape=[
             pltpu.VMEM((ports, 2 * LANES), jnp.float32),
@@ -273,7 +312,7 @@
             pltpu.VMEM((2 * times_count, LANES), jnp.float32),
         ],
         name="waves",
-    )(in_hbm(impedance), in_vmem(parts))
+    )(in_vmem(z), in_vmem(parts))
     columns = [
         [ports_count * t + 2 * x + c for t in range(times_count) for c in range(2)]
         for x in range(chips)
@@ -301,19 +340,12 @@
         means.append(lax.ppermute(mean, "port", ahead[k - 1]))
     return pl.pallas_call(
         scatter_body,
-        in_specs=[SMEM, SMEM] + [VMEM] * (chips + 3),
+        in_specs=[VMEM] * (chips + 4),
         out_specs=VMEM,
         out_shape=jax.ShapeDtypeStruct((2, ports, LANES), jnp.float32),
-        scratch_shapes=[
-            pltpu.VMEM((2, chips, ports, 2 * LANES), jnp.float32),
-            pltpu.VMEM((ports_count * ports, LANES), jnp.float32),
-            pltpu.VMEM((ports, 2 * LANES), jnp.float32),
-            pltpu.VMEM((ports, LANES), jnp.float32),
-        ],
         name="scatter",
     )(
-        lax.axis_index("port").reshape(1), in_hbm(pairing), in_vmem(same), in_vmem(other),
-        *map(in_vmem, means), in_vmem(own),
+        in_vmem(driven), in_vmem(same), in_vmem(other), *map(in_vmem, means), in_vmem(own),
     )
 
 

time: 64.2 us -> 62.7 us (0.977)
  Pallas kernels: 12.3 us -> 10.8 us
    pallas_call x1, Pallas kernels: 1.84 us -> 0.85 us  [body(): pl.pallas_call(scatter_body, in_specs=[VMEM] * (chips + 4), out_specs=VME...]
    pallas_call x1, Pallas kernels: 0.85 us -> 0.19 us  [body(): pl.pallas_call(functools.partial(waves_body, scale=1.0 / math.sqrt(total)...]
where the time goes in v5:
time: 62.7 us; the launch traced here: 62.5 us
  blocking collectives  36.2 us (58%)
  Pallas kernels  10.8 us (17%)
  waiting for transfers between devices  7.84 us (13%)
  starting transfers between devices  7.55 us (12%)
    all_to_all x1, blocking collectives, body(): parts = lax.all_to_all(in_vmem(parts), 'tm', 0, 0, tiled=True)  24.8 us
    all_to_all x1, blocking collectives, body(): lax.all_to_all(in_vmem(share), ('tm', 'port'), 0, 0, tiled=True, axis_ind...  11.4 us
    pallas_call x1, Pallas kernels, transform(): pl.pallas_call(functools.partial(transform_body, inner=INNER, total=total...  9.72 us
    ppermute x3, starting transfers between devices, body(): along.append(lax.ppermute(sent, 'port', ahead[k - 1]))  4.5 us
    ppermute x3, waiting for transfers between devices, body(): along.append(lax.ppermute(sent, 'port', ahead[k - 1]))  4.24 us
    ppermute x3, waiting for transfers between devices, body(): means.append(lax.ppermute(mean, 'port', ahead[k - 1]))  3.59 us
    ppermute x3, starting transfers between devices, body(): means.append(lax.ppermute(mean, 'port', ahead[k - 1]))  2.97 us
  transfers between devices with their start and end apart: 7, of which 5 were waited for; matrix products, arithmetic and copies ran while one was open for 0% of the time, Pallas kernels for 0%

profile of v5, /device:TPU:0, one launch (start us, length us, event | category | flops | bytes accessed | tf_op | source)
XLA Modules:
  0.0 62.5 jit_solution(4436963950711352171)
XLA Ops:
  0.0 9.7 %spectrum.1 = (f32[16,128,128]{2,1,0:T(8,128)S(1)}, f32[32,128]{1,0:T(8,128)S(1)}, s32[32,128]{1,0:T(8,128)S(1)}) custom-call(s32[32]{0:T(128)} %start_ref.1, f32[32]{0:T(128)} %impedance_ref.1, s32[32]{0:T(128)} %pairing_ref.1, s32[1,2048]{1,0:T(1,128)} %bitcast.15, f32[32,16384]{1,0:T(8,128)} %v_ref.1, f32[32,16384]{1,0:T(8,128)} %c_ref.1), custom_call_target="tpu_custom_call" | custom-call | tf_op jit(solution)/shard_map/spectrum/pallas_call | solution.py:188
  9.7 24.8 %all_to_all.16.parts_ref = f32[16,128,128]{2,1,0:T(8,128)S(1)} all-to-all(f32[16,128,128]{2,1,0:T(8,128)S(1)} %get-tuple-element.13), channel_id=1, replica_groups=mesh['tm'=16,'port'=8] {'tm'}, dimensions={0} | all-to-all | bytes 2097152 | tf_op jit(solution)/shard_map/all_to_all | solution.py:304
  34.6 0.2 waves.1
  34.7 2.8 %collective-permute-start.2 = (f32[32,256]{1,0:T(8,128)S(1)}, f32[32,256]{1,0:T(8,128)S(1)}, u32[]{:S(2)}, u32[]{:S(2)}) collective-permute-start(f32[32,256]{1,0:T(8,128)S(1)} %get-tuple-element.14), channel_id=1, source_target_pairs={{0,6},{1,7},{2,0},{3,1},{4,2},{5,3},{6,4},{7,5},{8,14},{9,15},{10,... | collective-permute-start | bytes 98312 | tf_op jit(solution)/shard_map/ppermute | solution.py:328
  37.6 0.8 %collective-permute-start.1 = (f32[32,256]{1,0:T(8,128)S(1)}, f32[32,256]{1,0:T(8,128)S(1)}, u32[]{:S(2)}, u32[]{:S(2)}) collective-permute-start(f32[32,256]{1,0:T(8,128)S(1)} %get-tuple-element.14), channel_id=1, source_target_pairs={{0,4},{1,5},{2,6},{3,7},{4,0},{5,1},{6,2},{7,3},{8,12},{9,13},{10,... | collective-permute-start | bytes 98312 | tf_op jit(solution)/shard_map/ppermute | solution.py:328
  38.4 0.9 %collective-permute-start = (f32[32,256]{1,0:T(8,128)S(1)}, f32[32,256]{1,0:T(8,128)S(1)}, u32[]{:S(2)}, u32[]{:S(2)}) collective-permute-start(f32[32,256]{1,0:T(8,128)S(1)} %get-tuple-element.14), channel_id=1, source_target_pairs={{0,2},{1,3},{2,4},{3,5},{4,6},{5,7},{6,0},{7,1},{8,10},{9,11},{10,... | collective-permute-start | bytes 98312 | tf_op jit(solution)/shard_map/ppermute | solution.py:328
  39.2 0.0 collective-permute-done.2
  39.2 3.8 %collective-permute-done.1 = f32[32,256]{1,0:T(8,128)S(1)} collective-permute-done((f32[32,256]{1,0:T(8,128)S(1)}, f32[32,256]{1,0:T(8,128)S(1)}, u32[]{:S(2)}, u32[]{:S(2)}) %collective-permute-start.1) | collective-permute-done | bytes 32800 | tf_op jit(solution)/shard_map/ppermute | solution.py:328
  43.0 0.5 collective-permute-done
  43.5 0.1 collective-permute-start.3
  43.6 11.4 %all_to_all.17 = f32[32,1,128]{2,1,0:T(1,128)S(1)} all-to-all(f32[32,1,128]{2,1,0:T(1,128)S(1)} %bitcast.11), channel_id=1, replica_groups={{0,1,8,9,16,17,24,25,32,33,40,41,48,49,56,57,64,65,72,73,80,81,88,89,96..., dimensions={0} | all-to-all | bytes 32768 | tf_op jit(solution)/shard_map/all_to_all | solution.py:323
  55.0 0.1 means.1.mean_0
  55.1 0.4 collective-permute-start.6
  55.5 1.3 %collective-permute-start.5 = (f32[8,128]{1,0:T(8,128)S(1)}, f32[8,128]{1,0:T(8,128)S(1)}, u32[]{:S(2)}, u32[]{:S(2)}) collective-permute-start(f32[8,128]{1,0:T(8,128)S(1)} %means.1.mean_0), channel_id=1, source_target_pairs={{0,4},{1,5},{2,6},{3,7},{4,0},{5,1},{6,2},{7,3},{8,12},{9,13},{10,... | collective-permute-start | bytes 12296 | tf_op jit(solution)/shard_map/ppermute | solution.py:340
  56.8 1.2 %collective-permute-start.4 = (f32[8,128]{1,0:T(8,128)S(1)}, f32[8,128]{1,0:T(8,128)S(1)}, u32[]{:S(2)}, u32[]{:S(2)}) collective-permute-start(f32[8,128]{1,0:T(8,128)S(1)} %means.1.mean_0), channel_id=1, source_target_pairs={{0,2},{1,3},{2,4},{3,5},{4,6},{5,7},{6,0},{7,1},{8,10},{9,11},{10,... | collective-permute-start | bytes 12296 | tf_op jit(solution)/shard_map/ppermute | solution.py:340
  58.1 0.6 %collective-permute-done.6.mean_3 = f32[8,128]{1,0:T(8,128)S(1)} collective-permute-done((f32[8,128]{1,0:T(8,128)S(1)}, f32[8,128]{1,0:T(8,128)S(1)}, u32[]{:S(2)}, u32[]{:S(2)}) %collective-permute-start.6) | collective-permute-done | bytes 4128 | tf_op jit(solution)/shard_map/ppermute | solution.py:340
  58.7 1.9 %collective-permute-done.5.mean_2 = f32[8,128]{1,0:T(8,128)S(1)} collective-permute-done((f32[8,128]{1,0:T(8,128)S(1)}, f32[8,128]{1,0:T(8,128)S(1)}, u32[]{:S(2)}, u32[]{:S(2)}) %collective-permute-start.5) | collective-permute-done | bytes 4128 | tf_op jit(solution)/shard_map/ppermute | solution.py:340
  60.6 1.0 %collective-permute-done.4.mean_1 = f32[8,128]{1,0:T(8,128)S(1)} collective-permute-done((f32[8,128]{1,0:T(8,128)S(1)}, f32[8,128]{1,0:T(8,128)S(1)}, u32[]{:S(2)}, u32[]{:S(2)}) %collective-permute-start.4) | collective-permute-done | bytes 4128 | tf_op jit(solution)/shard_map/ppermute | solution.py:340
  61.6 0.0 collective-permute-done.3.other_ref
  61.7 0.8 %scatter.1 = f32[2,32,128]{2,1,0:T(8,128)} custom-call(s32[32,128]{1,0:T(8,128)S(1)} %get-tuple-element.11.driven_ref, f32[4,32,256]{2,1,0:T(8,128)S(1)} %pad_maximum_fusion.same_ref, f32[4,32,256]{2,1,0:T(8,128)S(1)} %collective-permute-done.3.other_ref, f32[8,128]{1,0:T(8,128)S(1)} %means.1.mean_0, f32[8,128]{1,0:T(8,128)S(1)} %collective-permute-done.4.mean_1, ...), custom_call_target="tpu_custom_call" | custom-call | tf_op jit(solution)/shard_map/scatter/pallas_call | solution.py:341
  (1 shorter events, 0.0 us)
Async XLA Ops:
  34.7 4.5 %collective-permute-start.2 = (f32[32,256]{1,0:T(8,128)S(1)}, f32[32,256]{1,0:T(8,128)S(1)}, u32[]{:S(2)}, u32[]{:S(2)}) collective-permute-start(f32[32,256]{1,0:T(8,128)S(1)} %get-tuple-element.14), channel_id=1, source_target_pairs={{0,6},{1,7},{2,0},{3,1},{4,2},{5,3},{6,4},{7,5},{8,14},{9,15},{10,... | collective-permute-start | bytes 98312 | tf_op jit(solution)/shard_map/ppermute | solution.py:328
  37.6 5.4 %collective-permute-start.1 = (f32[32,256]{1,0:T(8,128)S(1)}, f32[32,256]{1,0:T(8,128)S(1)}, u32[]{:S(2)}, u32[]{:S(2)}) collective-permute-start(f32[32,256]{1,0:T(8,128)S(1)} %get-tuple-element.14), channel_id=1, source_target_pairs={{0,4},{1,5},{2,6},{3,7},{4,0},{5,1},{6,2},{7,3},{8,12},{9,13},{10,... | collective-permute-start | bytes 98312 | tf_op jit(solution)/shard_map/ppermute | solution.py:328
  38.4 5.1 %collective-permute-start = (f32[32,256]{1,0:T(8,128)S(1)}, f32[32,256]{1,0:T(8,128)S(1)}, u32[]{:S(2)}, u32[]{:S(2)}) collective-permute-start(f32[32,256]{1,0:T(8,128)S(1)} %get-tuple-element.14), channel_id=1, source_target_pairs={{0,2},{1,3},{2,4},{3,5},{4,6},{5,7},{6,0},{7,1},{8,10},{9,11},{10,... | collective-permute-start | bytes 98312 | tf_op jit(solution)/shard_map/ppermute | solution.py:328
  43.5 18.2 %collective-permute-start.3 = (f32[4,32,256]{2,1,0:T(8,128)S(1)}, f32[4,32,256]{2,1,0:T(8,128)S(1)}, u32[]{:S(2)}, u32[]{:S(2)}) collective-permute-start(f32[4,32,256]{2,1,0:T(8,128)S(1)} %pad_maximum_fusion.same_ref), channel_id=1, source_target_pairs={{0,1},{1,0},{2,3},{3,2},{4,5},{5,4},{6,7},{7,6},{8,9},{9,8},{10,11... | collective-permute-start | bytes 393224 | tf_op jit(solution)/shard_map/ppermute | solution.py:330
  55.1 3.6 %collective-permute-start.6 = (f32[8,128]{1,0:T(8,128)S(1)}, f32[8,128]{1,0:T(8,128)S(1)}, u32[]{:S(2)}, u32[]{:S(2)}) collective-permute-start(f32[8,128]{1,0:T(8,128)S(1)} %means.1.mean_0), channel_id=1, source_target_pairs={{0,6},{1,7},{2,0},{3,1},{4,2},{5,3},{6,4},{7,5},{8,14},{9,15},{10,... | collective-permute-start | bytes 12296 | tf_op jit(solution)/shard_map/ppermute | solution.py:340
  55.5 5.1 %collective-permute-start.5 = (f32[8,128]{1,0:T(8,128)S(1)}, f32[8,128]{1,0:T(8,128)S(1)}, u32[]{:S(2)}, u32[]{:S(2)}) collective-permute-start(f32[8,128]{1,0:T(8,128)S(1)} %means.1.mean_0), channel_id=1, source_target_pairs={{0,4},{1,5},{2,6},{3,7},{4,0},{5,1},{6,2},{7,3},{8,12},{9,13},{10,... | collective-permute-start | bytes 12296 | tf_op jit(solution)/shard_map/ppermute | solution.py:340
  56.8 4.8 %collective-permute-start.4 = (f32[8,128]{1,0:T(8,128)S(1)}, f32[8,128]{1,0:T(8,128)S(1)}, u32[]{:S(2)}, u32[]{:S(2)}) collective-permute-start(f32[8,128]{1,0:T(8,128)S(1)} %means.1.mean_0), channel_id=1, source_target_pairs={{0,2},{1,3},{2,4},{3,5},{4,6},{5,7},{6,0},{7,1},{8,10},{9,11},{10,... | collective-permute-start | bytes 12296 | tf_op jit(solution)/shard_map/ppermute | solution.py:340

commit v6 on v5

--- a/solution.py
+++ b/solution.py
@@ -13,6 +13,7 @@
 COLUMNS = 256
 INNER = 1024
 FLIP = 256
+BLOCK = 16
 VMEM = pl.BlockSpec(memory_space=pltpu.VMEM)
 HBM = pl.BlockSpec(memory_space=pltpu.HBM)
 
@@ -107,31 +108,35 @@
             sin_ref[at] = (sin_u * fine_cos + cos_u * fine_sin).astype(jnp.bfloat16)
 
     def spectra(cos_ref, sin_ref, turn_ref, base):
-        group = max(1, 512 // both)
-        re = jnp.zeros((both, cols), jnp.float32)
-        im = jnp.zeros((both, cols), jnp.float32)
-        for g in range(0, outer, group):
-            at = slice(g * both, (g + group) * both)
+        deep = outer * BLOCK
+        group = max(1, 1024 // deep)
+        for g in range(0, both // BLOCK, group):
+            at = slice(g * deep, (g + group) * deep)
             part_re = jnp.dot(even_ref[at], cos_ref[...], preferred_element_type=jnp.float32)
             part_im = jnp.dot(odd_ref[at], sin_ref[...], preferred_element_type=jnp.float32)
-            for s in range(group):
-                re_s = part_re[s * both : (s + 1) * both]
-                im_s = part_im[s * both : (s + 1) * both]
-                cos_s = turn_ref[g + s : g + s + 1]
-                sin_s = turn_ref[outer + g + s : outer + g + s + 1]
-                re = re + (re_s * cos_s - im_s * sin_s)
-                im = im + (re_s * sin_s + im_s * cos_s)
-        for j in range(cols // LANES):
-            at = slice(j * LANES, (j + 1) * LANES)
-            out_ref[base + j, :both] = re[:, at]
-            out_ref[base + j, both:] = im[:, at]
+            for b in range(group):
+                re = jnp.zeros((BLOCK, cols), jnp.float32)
+                im = jnp.zeros((BLOCK, cols), jnp.float32)
+                for s in range(outer):
+                    low = b * deep + s * BLOCK
+                    re_s = part_re[low : low + BLOCK]
+                    im_s = part_im[low : low + BLOCK]
+                    cos_s = turn_ref[s : s + 1]
+                    sin_s = turn_ref[outer + s : outer + s + 1]
+                    re = re + (re_s * cos_s - im_s * sin_s)
+                    im = im + (re_s * sin_s + im_s * cos_s)
+                low = (g + b) * BLOCK
+                for j in range(cols // LANES):
+                    at = slice(j * LANES, (j + 1) * LANES)
+                    out_ref[base + j, low : low + BLOCK] = re[:, at]
+                    out_ref[base + j, both + low : both + low + BLOCK] = im[:, at]
 
     @pl.when(step == 0)
     def _():
         small[0].start()
         for s in range(outer):
             for copy in copies(s):
-                copy.start()
+                copy.start(priority=1)
         for copy in small[1:]:
             copy.start()
         small[0].wait()
@@ -144,31 +149,37 @@
         row = lax.broadcasted_iota(jnp.int32, (FLIP, FLIP), 0)
         col = lax.broadcasted_iota(jnp.int32, (FLIP, FLIP), 1)
         flip = jnp.where(row + col == FLIP - 1, 1.0, 0.0).astype(jnp.bfloat16)
-        group = max(1, 256 // both)
+        deep = outer * BLOCK
+        group = max(1, 512 // both)
         for g in range(0, outer, group):
             for s in range(g, g + group):
                 at = slice(s * inner, (s + 1) * inner)
                 time = first + s * inner
                 time = time + lax.broadcasted_iota(jnp.int32, (ports, inner), 1)
                 keep = time >= start
-                low = s * both
                 for copy in copies(s):
                     copy.wait()
-                raw_ref[low : low + ports] = jnp.where(keep, v_in[:, at], 0.0).astype(jnp.bfloat16)
-                raw_ref[low + ports : low + both] = jnp.where(keep, c_in[:, at], 0.0).astype(
-                    jnp.bfloat16
-                )
-            at = slice(g * both, (g + group) * both)
-            for q in range(half // FLIP):
-                to = slice(q * FLIP, (q + 1) * FLIP)
-                behind = jnp.dot(
-                    raw_ref[at, half - (q + 1) * FLIP : half - q * FLIP],
-                    flip,
-                    preferred_element_type=jnp.float32,
-                )
-                ahead = raw_ref[at, half + q * FLIP : half + (q + 1) * FLIP].astype(jnp.float32)
-                even_ref[at, to] = (ahead + behind).astype(jnp.bfloat16)
-                odd_ref[at, to] = (ahead - behind).astype(jnp.bfloat16)
+                gated_v = jnp.where(keep, v_in[:, at], 0.0).astype(jnp.bfloat16)
+                gated_c = jnp.where(keep, c_in[:, at], 0.0).astype(jnp.bfloat16)
+                for b in range(ports // BLOCK):
+                    of = slice(b * BLOCK, (b + 1) * BLOCK)
+                    low = b * deep + s * BLOCK
+                    raw_ref[low : low + BLOCK] = gated_v[of]
+                    low += ports // BLOCK * deep
+                    raw_ref[low : low + BLOCK] = gated_c[of]
+            for b in range(both // BLOCK):
+                at = slice(b * deep + g * BLOCK, b * deep + (g + group) * BLOCK)
+                for q in range(half // FLIP):
+                    to = slice(q * FLIP, (q + 1) * FLIP)
+                    behind = jnp.dot(
+                        raw_ref[at, half - (q + 1) * FLIP : half - q * FLIP],
+                        flip,
+                        preferred_element_type=jnp.float32,
+                    )
+                    ahead = raw_ref[at, half + q * FLIP : half + (q + 1) * FLIP]
+                    ahead = ahead.astype(jnp.float32)
+                    even_ref[at, to] = (ahead + behind).astype(jnp.bfloat16)
+                    odd_ref[at, to] = (ahead - behind).astype(jnp.bfloat16)
 
     build(lines_of(2 * step + 1), cos_1, sin_1, turn_1)
     spectra(cos_0, sin_0, turn_0, 0)

time: 62.7 us -> 61.4 us (0.979)
  Pallas kernels: 10.8 us -> 9.51 us
    pallas_call x1, Pallas kernels: 9.72 us -> 8.39 us  [transform(): pl.pallas_call(functools.partial(transform_body, inner=INNER, total=total...]
where the time goes in v6:
time: 61.4 us; the launch traced here: 61.2 us
  blocking collectives  36.2 us (59%)
  Pallas kernels  9.51 us (15%)
  waiting for transfers between devices  7.85 us (13%)
  starting transfers between devices  7.57 us (12%)
    all_to_all x1, blocking collectives, body(): parts = lax.all_to_all(in_vmem(parts), 'tm', 0, 0, tiled=True)  24.8 us
    all_to_all x1, blocking collectives, body(): lax.all_to_all(in_vmem(share), ('tm', 'port'), 0, 0, tiled=True, axis_ind...  11.4 us
    pallas_call x1, Pallas kernels, transform(): pl.pallas_call(functools.partial(transform_body, inner=INNER, total=total...  8.39 us
    ppermute x3, starting transfers between devices, body(): along.append(lax.ppermute(sent, 'port', ahead[k - 1]))  4.53 us
    ppermute x3, waiting for transfers between devices, body(): along.append(lax.ppermute(sent, 'port', ahead[k - 1]))  4.22 us
    ppermute x3, waiting for transfers between devices, body(): means.append(lax.ppermute(mean, 'port', ahead[k - 1]))  3.63 us
    ppermute x3, starting transfers between devices, body(): means.append(lax.ppermute(mean, 'port', ahead[k - 1]))  2.95 us
  transfers between devices with their start and end apart: 7, of which 5 were waited for; matrix products, arithmetic and copies ran while one was open for 0% of the time, Pallas kernels for 0%

profile of v6, /device:TPU:0, one launch (start us, length us, event | category | flops | bytes accessed | tf_op | source)
XLA Modules:
  0.0 61.2 jit_solution(16481295176028819133)
XLA Ops:
  0.0 8.4 %spectrum.1 = (f32[16,128,128]{2,1,0:T(8,128)S(1)}, f32[32,128]{1,0:T(8,128)S(1)}, s32[32,128]{1,0:T(8,128)S(1)}) custom-call(s32[32]{0:T(128)} %start_ref.1, f32[32]{0:T(128)} %impedance_ref.1, s32[32]{0:T(128)} %pairing_ref.1, s32[1,2048]{1,0:T(1,128)} %bitcast.15, f32[32,16384]{1,0:T(8,128)} %v_ref.1, f32[32,16384]{1,0:T(8,128)} %c_ref.1), custom_call_target="tpu_custom_call" | custom-call | tf_op jit(solution)/shard_map/spectrum/pallas_call | solution.py:199
  8.4 24.8 %all_to_all.16.parts_ref = f32[16,128,128]{2,1,0:T(8,128)S(1)} all-to-all(f32[16,128,128]{2,1,0:T(8,128)S(1)} %get-tuple-element.13), channel_id=1, replica_groups=mesh['tm'=16,'port'=8] {'tm'}, dimensions={0} | all-to-all | bytes 2097152 | tf_op jit(solution)/shard_map/all_to_all | solution.py:315
  33.2 0.2 waves.1
  33.4 2.8 %collective-permute-start.2 = (f32[32,256]{1,0:T(8,128)S(1)}, f32[32,256]{1,0:T(8,128)S(1)}, u32[]{:S(2)}, u32[]{:S(2)}) collective-permute-start(f32[32,256]{1,0:T(8,128)S(1)} %get-tuple-element.14), channel_id=1, source_target_pairs={{0,6},{1,7},{2,0},{3,1},{4,2},{5,3},{6,4},{7,5},{8,14},{9,15},{10,... | collective-permute-start | bytes 98312 | tf_op jit(solution)/shard_map/ppermute | solution.py:339
  36.2 0.8 %collective-permute-start.1 = (f32[32,256]{1,0:T(8,128)S(1)}, f32[32,256]{1,0:T(8,128)S(1)}, u32[]{:S(2)}, u32[]{:S(2)}) collective-permute-start(f32[32,256]{1,0:T(8,128)S(1)} %get-tuple-element.14), channel_id=1, source_target_pairs={{0,4},{1,5},{2,6},{3,7},{4,0},{5,1},{6,2},{7,3},{8,12},{9,13},{10,... | collective-permute-start | bytes 98312 | tf_op jit(solution)/shard_map/ppermute | solution.py:339
  37.0 0.9 %collective-permute-start = (f32[32,256]{1,0:T(8,128)S(1)}, f32[32,256]{1,0:T(8,128)S(1)}, u32[]{:S(2)}, u32[]{:S(2)}) collective-permute-start(f32[32,256]{1,0:T(8,128)S(1)} %get-tuple-element.14), channel_id=1, source_target_pairs={{0,2},{1,3},{2,4},{3,5},{4,6},{5,7},{6,0},{7,1},{8,10},{9,11},{10,... | collective-permute-start | bytes 98312 | tf_op jit(solution)/shard_map/ppermute | solution.py:339
  37.9 0.0 collective-permute-done.2
  37.9 3.7 %collective-permute-done.1 = f32[32,256]{1,0:T(8,128)S(1)} collective-permute-done((f32[32,256]{1,0:T(8,128)S(1)}, f32[32,256]{1,0:T(8,128)S(1)}, u32[]{:S(2)}, u32[]{:S(2)}) %collective-permute-start.1) | collective-permute-done | bytes 32800 | tf_op jit(solution)/shard_map/ppermute | solution.py:339
  41.6 0.5 collective-permute-done
  42.1 0.1 collective-permute-start.3
  42.2 11.4 %all_to_all.17 = f32[32,1,128]{2,1,0:T(1,128)S(1)} all-to-all(f32[32,1,128]{2,1,0:T(1,128)S(1)} %bitcast.11), channel_id=1, replica_groups={{0,1,8,9,16,17,24,25,32,33,40,41,48,49,56,57,64,65,72,73,80,81,88,89,96..., dimensions={0} | all-to-all | bytes 32768 | tf_op jit(solution)/shard_map/all_to_all | solution.py:334
  53.7 0.1 means.1.mean_0
  53.7 0.4 collective-permute-start.6
  54.2 1.3 %collective-permute-start.5 = (f32[8,128]{1,0:T(8,128)S(1)}, f32[8,128]{1,0:T(8,128)S(1)}, u32[]{:S(2)}, u32[]{:S(2)}) collective-permute-start(f32[8,128]{1,0:T(8,128)S(1)} %means.1.mean_0), channel_id=1, source_target_pairs={{0,4},{1,5},{2,6},{3,7},{4,0},{5,1},{6,2},{7,3},{8,12},{9,13},{10,... | collective-permute-start | bytes 12296 | tf_op jit(solution)/shard_map/ppermute | solution.py:351
  55.5 1.2 %collective-permute-start.4 = (f32[8,128]{1,0:T(8,128)S(1)}, f32[8,128]{1,0:T(8,128)S(1)}, u32[]{:S(2)}, u32[]{:S(2)}) collective-permute-start(f32[8,128]{1,0:T(8,128)S(1)} %means.1.mean_0), channel_id=1, source_target_pairs={{0,2},{1,3},{2,4},{3,5},{4,6},{5,7},{6,0},{7,1},{8,10},{9,11},{10,... | collective-permute-start | bytes 12296 | tf_op jit(solution)/shard_map/ppermute | solution.py:351
  56.7 0.7 %collective-permute-done.6.mean_3 = f32[8,128]{1,0:T(8,128)S(1)} collective-permute-done((f32[8,128]{1,0:T(8,128)S(1)}, f32[8,128]{1,0:T(8,128)S(1)}, u32[]{:S(2)}, u32[]{:S(2)}) %collective-permute-start.6) | collective-permute-done | bytes 4128 | tf_op jit(solution)/shard_map/ppermute | solution.py:351
  57.4 1.9 %collective-permute-done.5.mean_2 = f32[8,128]{1,0:T(8,128)S(1)} collective-permute-done((f32[8,128]{1,0:T(8,128)S(1)}, f32[8,128]{1,0:T(8,128)S(1)}, u32[]{:S(2)}, u32[]{:S(2)}) %collective-permute-start.5) | collective-permute-done | bytes 4128 | tf_op jit(solution)/shard_map/ppermute | solution.py:351
  59.3 1.1 %collective-permute-done.4.mean_1 = f32[8,128]{1,0:T(8,128)S(1)} collective-permute-done((f32[8,128]{1,0:T(8,128)S(1)}, f32[8,128]{1,0:T(8,128)S(1)}, u32[]{:S(2)}, u32[]{:S(2)}) %collective-permute-start.4) | collective-permute-done | bytes 4128 | tf_op jit(solution)/shard_map/ppermute | solution.py:351
  60.3 0.0 collective-permute-done.3.other_ref
  60.3 0.8 %scatter.1 = f32[2,32,128]{2,1,0:T(8,128)} custom-call(s32[32,128]{1,0:T(8,128)S(1)} %get-tuple-element.11.driven_ref, f32[4,32,256]{2,1,0:T(8,128)S(1)} %pad_maximum_fusion.same_ref, f32[4,32,256]{2,1,0:T(8,128)S(1)} %collective-permute-done.3.other_ref, f32[8,128]{1,0:T(8,128)S(1)} %means.1.mean_0, f32[8,128]{1,0:T(8,128)S(1)} %collective-permute-done.4.mean_1, ...), custom_call_target="tpu_custom_call" | custom-call | tf_op jit(solution)/shard_map/scatter/pallas_call | solution.py:352
  (1 shorter events, 0.0 us)
Async XLA Ops:
  33.4 4.5 %collective-permute-start.2 = (f32[32,256]{1,0:T(8,128)S(1)}, f32[32,256]{1,0:T(8,128)S(1)}, u32[]{:S(2)}, u32[]{:S(2)}) collective-permute-start(f32[32,256]{1,0:T(8,128)S(1)} %get-tuple-element.14), channel_id=1, source_target_pairs={{0,6},{1,7},{2,0},{3,1},{4,2},{5,3},{6,4},{7,5},{8,14},{9,15},{10,... | collective-permute-start | bytes 98312 | tf_op jit(solution)/shard_map/ppermute | solution.py:339
  36.2 5.4 %collective-permute-start.1 = (f32[32,256]{1,0:T(8,128)S(1)}, f32[32,256]{1,0:T(8,128)S(1)}, u32[]{:S(2)}, u32[]{:S(2)}) collective-permute-start(f32[32,256]{1,0:T(8,128)S(1)} %get-tuple-element.14), channel_id=1, source_target_pairs={{0,4},{1,5},{2,6},{3,7},{4,0},{5,1},{6,2},{7,3},{8,12},{9,13},{10,... | collective-permute-start | bytes 98312 | tf_op jit(solution)/shard_map/ppermute | solution.py:339
  37.0 5.1 %collective-permute-start = (f32[32,256]{1,0:T(8,128)S(1)}, f32[32,256]{1,0:T(8,128)S(1)}, u32[]{:S(2)}, u32[]{:S(2)}) collective-permute-start(f32[32,256]{1,0:T(8,128)S(1)} %get-tuple-element.14), channel_id=1, source_target_pairs={{0,2},{1,3},{2,4},{3,5},{4,6},{5,7},{6,0},{7,1},{8,10},{9,11},{10,... | collective-permute-start | bytes 98312 | tf_op jit(solution)/shard_map/ppermute | solution.py:339
  42.1 18.2 %collective-permute-start.3 = (f32[4,32,256]{2,1,0:T(8,128)S(1)}, f32[4,32,256]{2,1,0:T(8,128)S(1)}, u32[]{:S(2)}, u32[]{:S(2)}) collective-permute-start(f32[4,32,256]{2,1,0:T(8,128)S(1)} %pad_maximum_fusion.same_ref), channel_id=1, source_target_pairs={{0,1},{1,0},{2,3},{3,2},{4,5},{5,4},{6,7},{7,6},{8,9},{9,8},{10,11... | collective-permute-start | bytes 393224 | tf_op jit(solution)/shard_map/ppermute | solution.py:341
  53.7 3.6 %collective-permute-start.6 = (f32[8,128]{1,0:T(8,128)S(1)}, f32[8,128]{1,0:T(8,128)S(1)}, u32[]{:S(2)}, u32[]{:S(2)}) collective-permute-start(f32[8,128]{1,0:T(8,128)S(1)} %means.1.mean_0), channel_id=1, source_target_pairs={{0,6},{1,7},{2,0},{3,1},{4,2},{5,3},{6,4},{7,5},{8,14},{9,15},{10,... | collective-permute-start | bytes 12296 | tf_op jit(solution)/shard_map/ppermute | solution.py:351
  54.2 5.1 %collective-permute-start.5 = (f32[8,128]{1,0:T(8,128)S(1)}, f32[8,128]{1,0:T(8,128)S(1)}, u32[]{:S(2)}, u32[]{:S(2)}) collective-permute-start(f32[8,128]{1,0:T(8,128)S(1)} %means.1.mean_0), channel_id=1, source_target_pairs={{0,4},{1,5},{2,6},{3,7},{4,0},{5,1},{6,2},{7,3},{8,12},{9,13},{10,... | collective-permute-start | bytes 12296 | tf_op jit(solution)/shard_map/ppermute | solution.py:351
  55.5 4.8 %collective-permute-start.4 = (f32[8,128]{1,0:T(8,128)S(1)}, f32[8,128]{1,0:T(8,128)S(1)}, u32[]{:S(2)}, u32[]{:S(2)}) collective-permute-start(f32[8,128]{1,0:T(8,128)S(1)} %means.1.mean_0), channel_id=1, source_target_pairs={{0,2},{1,3},{2,4},{3,5},{4,6},{5,7},{6,0},{7,1},{8,10},{9,11},{10,... | collective-permute-start | bytes 12296 | tf_op jit(solution)/shard_map/ppermute | solution.py:351

commit v7 on v6

--- a/solution.py
+++ b/solution.py
@@ -98,7 +98,15 @@
         fine = 16
         coarse = half // fine
         fine_cos, fine_sin = turned(lines * (2 * steps(fine) + 1), 2 * total)
-        coarse_cos, coarse_sin = turned(lines * (steps(coarse) * (2 * fine)), 2 * total)
+        near_cos, near_sin = turned(lines * (steps(8) * (2 * fine)), 2 * total)
+        far_cos, far_sin = turned(lines * (steps(coarse // 8) * (16 * fine)), 2 * total)
+        coarse_cos, coarse_sin = [], []
+        for u in range(coarse // 8):
+            cos_u, sin_u = far_cos[u : u + 1], far_sin[u : u + 1]
+            coarse_cos.append(cos_u * near_cos - sin_u * near_sin)
+            coarse_sin.append(sin_u * near_cos + cos_u * near_sin)
+        coarse_cos = jnp.concatenate(coarse_cos, axis=0)
+        coarse_sin = jnp.concatenate(coarse_sin, axis=0)
         middle = 2 * (first + steps(outer) * inner + half) - 1
         turn_ref[:outer], turn_ref[outer:] = turned(lines * middle, 2 * total)
         for u in range(coarse):
@@ -181,10 +189,10 @@
                     even_ref[at, to] = (ahead + behind).astype(jnp.bfloat16)
                     odd_ref[at, to] = (ahead - behind).astype(jnp.bfloat16)
 
+    spectra(cos_0, sin_0, turn_0, 0)
     build(lines_of(2 * step + 1), cos_1, sin_1, turn_1)
-    spectra(cos_0, sin_0, turn_0, 0)
+    spectra(cos_1, sin_1, turn_1, cols // LANES)
     build(lines_of(2 * jnp.minimum(step + 1, steps_count - 1)), cos_0, sin_0, turn_0)
-    spectra(cos_1, sin_1, turn_1, cols // LANES)
 
 
 def transform(start, impedance, pairing, freq_index, voltages, currents, total):
@@ -258,21 +266,12 @@
     share_ref[...] = jnp.broadcast_to(share, share_ref.shape)
 
 
-def means_body(shares_ref, out_ref, *, ports, width):
-    row = lax.broadcasted_iota(jnp.int32, shares_ref.shape, 0)
-    shares = shares_ref[...]
-    lane = lax.broadcasted_iota(jnp.int32, (1, LANES), 1)
-    sums = [
-        jnp.sum(jnp.where((row & 1) == c, shares, 0.0), axis=0, keepdims=True) for c in range(2)
-    ]
-    both = jnp.where(lane < ports, sums[0], pltpu.roll(sums[1], ports, 1))
-    out_ref[...] = jnp.broadcast_to(both / width + 1e-06, out_ref.shape)
-
-
-def scatter_body(driven_ref, same_ref, other_ref, mean_0, mean_1, mean_2, mean_3, own_ref, out_ref):
+def scatter_body(
+    driven_ref, same_ref, other_ref, share_0, share_1, share_2, share_3, own_ref, out_ref, *, width
+):
     ports = own_ref.shape[0]
-    means = (mean_0, mean_1, mean_2, mean_3)
-    chips = len(means)
+    shares = (share_0, share_1, share_2, share_3)
+    chips = len(shares)
     place = lax.axis_index("port")
     driven = driven_ref[...]
     holder = driven // ports
@@ -291,10 +290,13 @@
             q = q + jnp.dot(picks, term, preferred_element_type=jnp.float32)
             left = left - term.astype(jnp.float32)
     level = jnp.zeros((ports, LANES), jnp.float32)
+    sender = lax.broadcasted_iota(jnp.int32, share_0.shape, 0) & 1
     for k in range(chips):
-        here = (lane == core * ports + rest) & (back == k)
-        level = level + jnp.where(here, means[k][:1], 0.0)
-    mean = jnp.sum(level, axis=1, keepdims=True)
+        for c in range(2):
+            summed = jnp.where(sender == c, shares[k][...], 0.0)
+            summed = jnp.sum(summed, axis=0, keepdims=True)
+            level = level + jnp.where((lane == rest) & (back == k) & (core == c), summed, 0.0)
+    mean = jnp.sum(level, axis=1, keepdims=True) / width + 1e-06
     q_re, q_im = q[:, :LANES], q[:, LANES:]
     b_re, b_im = own_ref[:, :LANES], own_ref[:, LANES:]
     power = q_re * q_re + q_im * q_im
@@ -339,18 +341,11 @@
         along.append(lax.ppermute(sent, "port", ahead[k - 1]))
     same = jnp.stack(along)
     other = lax.ppermute(same, "port", [(i, i ^ 1) for i in range(ports_count)])
-    mean = pl.pallas_call(
-        functools.partial(means_body, ports=ports, width=width),
-        in_specs=[VMEM],
-        out_specs=VMEM,
-        out_shape=pltpu.VMEM((8, LANES), jnp.float32),
-        name="means",
-    )(in_vmem(shares))
-    means = [mean]
+    means = [shares]
     for k in range(1, chips):
-        means.append(lax.ppermute(mean, "port", ahead[k - 1]))
+        means.append(lax.ppermute(shares, "port", ahead[k - 1]))
     return pl.pallas_call(
-        scatter_body,
+        functools.partial(scatter_body, width=width),
         in_specs=[VMEM] * (chips + 4),
         out_specs=VMEM,
         out_shape=jax.ShapeDtypeStruct((2, ports, LANES), jnp.float32),

time: 61.4 us -> 61.3 us (level)
  no operation moved by 1% of the time
where the time goes in v7:
time: 61.3 us; the launch traced here: 61.1 us
  blocking collectives  36.2 us (59%)
  Pallas kernels  9.33 us (15%)
  waiting for transfers between devices  7.99 us (13%)
  starting transfers between devices  7.54 us (12%)
    all_to_all x1, blocking collectives, body(): parts = lax.all_to_all(in_vmem(parts), 'tm', 0, 0, tiled=True)  24.8 us
    all_to_all x1, blocking collectives, body(): lax.all_to_all(in_vmem(share), ('tm', 'port'), 0, 0, tiled=True, axis_ind...  11.4 us
    pallas_call x1, Pallas kernels, transform(): pl.pallas_call(functools.partial(transform_body, inner=INNER, total=total...  8.3 us
    ppermute x3, starting transfers between devices, body(): along.append(lax.ppermute(sent, 'port', ahead[k - 1]))  4.51 us
    ppermute x3, waiting for transfers between devices, body(): along.append(lax.ppermute(sent, 'port', ahead[k - 1]))  4.24 us
    ppermute x3, waiting for transfers between devices, body(): means.append(lax.ppermute(shares, 'port', ahead[k - 1]))  3.75 us
    ppermute x3, starting transfers between devices, body(): means.append(lax.ppermute(shares, 'port', ahead[k - 1]))  2.94 us
  transfers between devices with their start and end apart: 7, of which 5 were waited for; matrix products, arithmetic and copies ran while one was open for 0% of the time, Pallas kernels for 0%

profile of v7, /device:TPU:0, one launch (start us, length us, event | category | flops | bytes accessed | tf_op | source)
XLA Modules:
  0.0 61.1 jit_solution(15355949245569340871)
XLA Ops:
  0.0 8.3 %spectrum.1 = (f32[16,128,128]{2,1,0:T(8,128)S(1)}, f32[32,128]{1,0:T(8,128)S(1)}, s32[32,128]{1,0:T(8,128)S(1)}) custom-call(s32[32]{0:T(128)} %start_ref.1, f32[32]{0:T(128)} %impedance_ref.1, s32[32]{0:T(128)} %pairing_ref.1, s32[1,2048]{1,0:T(1,128)} %bitcast.18, f32[32,16384]{1,0:T(8,128)} %v_ref.1, f32[32,16384]{1,0:T(8,128)} %c_ref.1), custom_call_target="tpu_custom_call" | custom-call | tf_op jit(solution)/shard_map/spectrum/pallas_call | solution.py:207
  8.3 24.8 %all_to_all.16.parts_ref = f32[16,128,128]{2,1,0:T(8,128)S(1)} all-to-all(f32[16,128,128]{2,1,0:T(8,128)S(1)} %get-tuple-element.13), channel_id=1, replica_groups=mesh['tm'=16,'port'=8] {'tm'}, dimensions={0} | all-to-all | bytes 2097152 | tf_op jit(solution)/shard_map/all_to_all | solution.py:317
  33.1 0.2 waves.1
  33.3 2.8 %collective-permute-start.2 = (f32[32,256]{1,0:T(8,128)S(1)}, f32[32,256]{1,0:T(8,128)S(1)}, u32[]{:S(2)}, u32[]{:S(2)}) collective-permute-start(f32[32,256]{1,0:T(8,128)S(1)} %get-tuple-element.14), channel_id=1, source_target_pairs={{0,6},{1,7},{2,0},{3,1},{4,2},{5,3},{6,4},{7,5},{8,14},{9,15},{10,... | collective-permute-start | bytes 98312 | tf_op jit(solution)/shard_map/ppermute | solution.py:341
  36.1 0.8 %collective-permute-start.1 = (f32[32,256]{1,0:T(8,128)S(1)}, f32[32,256]{1,0:T(8,128)S(1)}, u32[]{:S(2)}, u32[]{:S(2)}) collective-permute-start(f32[32,256]{1,0:T(8,128)S(1)} %get-tuple-element.14), channel_id=1, source_target_pairs={{0,4},{1,5},{2,6},{3,7},{4,0},{5,1},{6,2},{7,3},{8,12},{9,13},{10,... | collective-permute-start | bytes 98312 | tf_op jit(solution)/shard_map/ppermute | solution.py:341
  36.9 0.9 %collective-permute-start = (f32[32,256]{1,0:T(8,128)S(1)}, f32[32,256]{1,0:T(8,128)S(1)}, u32[]{:S(2)}, u32[]{:S(2)}) collective-permute-start(f32[32,256]{1,0:T(8,128)S(1)} %get-tuple-element.14), channel_id=1, source_target_pairs={{0,2},{1,3},{2,4},{3,5},{4,6},{5,7},{6,0},{7,1},{8,10},{9,11},{10,... | collective-permute-start | bytes 98312 | tf_op jit(solution)/shard_map/ppermute | solution.py:341
  37.8 0.0 collective-permute-done.2
  37.8 3.7 %collective-permute-done.1 = f32[32,256]{1,0:T(8,128)S(1)} collective-permute-done((f32[32,256]{1,0:T(8,128)S(1)}, f32[32,256]{1,0:T(8,128)S(1)}, u32[]{:S(2)}, u32[]{:S(2)}) %collective-permute-start.1) | collective-permute-done | bytes 32800 | tf_op jit(solution)/shard_map/ppermute | solution.py:341
  41.5 0.5 collective-permute-done
  42.1 0.1 collective-permute-start.3
  42.2 11.4 %all_to_all.17 = f32[32,1,128]{2,1,0:T(1,128)S(1)} all-to-all(f32[32,1,128]{2,1,0:T(1,128)S(1)} %bitcast.14), channel_id=1, replica_groups={{0,1,8,9,16,17,24,25,32,33,40,41,48,49,56,57,64,65,72,73,80,81,88,89,96..., dimensions={0} | all-to-all | bytes 32768 | tf_op jit(solution)/shard_map/all_to_all | solution.py:336
  53.6 0.4 collective-permute-start.6
  54.0 1.3 %collective-permute-start.5 = (f32[32,128]{1,0:T(8,128)S(1)}, f32[32,128]{1,0:T(8,128)S(1)}, u32[]{:S(2)}, u32[]{:S(2)}) collective-permute-start(f32[32,128]{1,0:T(8,128)S(1)} %bitcast.10), channel_id=1, source_target_pairs={{0,4},{1,5},{2,6},{3,7},{4,0},{5,1},{6,2},{7,3},{8,12},{9,13},{10,... | collective-permute-start | bytes 49160 | tf_op jit(solution)/shard_map/ppermute | solution.py:346
  55.3 1.2 %collective-permute-start.4 = (f32[32,128]{1,0:T(8,128)S(1)}, f32[32,128]{1,0:T(8,128)S(1)}, u32[]{:S(2)}, u32[]{:S(2)}) collective-permute-start(f32[32,128]{1,0:T(8,128)S(1)} %bitcast.11), channel_id=1, source_target_pairs={{0,2},{1,3},{2,4},{3,5},{4,6},{5,7},{6,0},{7,1},{8,10},{9,11},{10,... | collective-permute-start | bytes 49160 | tf_op jit(solution)/shard_map/ppermute | solution.py:346
  56.5 0.8 %collective-permute-done.6.share_3 = f32[32,128]{1,0:T(8,128)S(1)} collective-permute-done((f32[32,128]{1,0:T(8,128)S(1)}, f32[32,128]{1,0:T(8,128)S(1)}, u32[]{:S(2)}, u32[]{:S(2)}) %collective-permute-start.6) | collective-permute-done | bytes 16416 | tf_op jit(solution)/shard_map/ppermute | solution.py:346
  57.3 1.9 %collective-permute-done.5.share_2 = f32[32,128]{1,0:T(8,128)S(1)} collective-permute-done((f32[32,128]{1,0:T(8,128)S(1)}, f32[32,128]{1,0:T(8,128)S(1)}, u32[]{:S(2)}, u32[]{:S(2)}) %collective-permute-start.5) | collective-permute-done | bytes 16416 | tf_op jit(solution)/shard_map/ppermute | solution.py:346
  59.2 1.0 %collective-permute-done.4.share_1 = f32[32,128]{1,0:T(8,128)S(1)} collective-permute-done((f32[32,128]{1,0:T(8,128)S(1)}, f32[32,128]{1,0:T(8,128)S(1)}, u32[]{:S(2)}, u32[]{:S(2)}) %collective-permute-start.4) | collective-permute-done | bytes 16416 | tf_op jit(solution)/shard_map/ppermute | solution.py:346
  60.3 0.0 collective-permute-done.3.other_ref
  60.3 0.8 %scatter.1 = f32[2,32,128]{2,1,0:T(8,128)} custom-call(s32[32,128]{1,0:T(8,128)S(1)} %get-tuple-element.11.driven_ref, f32[4,32,256]{2,1,0:T(8,128)S(1)} %pad_maximum_fusion.same_ref, f32[4,32,256]{2,1,0:T(8,128)S(1)} %collective-permute-done.3.other_ref, f32[32,128]{1,0:T(8,128)S(1)} %bitcast.12, f32[32,128]{1,0:T(8,128)S(1)} %collective-permute-done.4.share_1, ...), custom_call_target="tpu_custom_call" | custom-call | tf_op jit(solution)/shard_map/scatter/pallas_call | solution.py:347
  (1 shorter events, 0.0 us)
Async XLA Ops:
  33.3 4.5 %collective-permute-start.2 = (f32[32,256]{1,0:T(8,128)S(1)}, f32[32,256]{1,0:T(8,128)S(1)}, u32[]{:S(2)}, u32[]{:S(2)}) collective-permute-start(f32[32,256]{1,0:T(8,128)S(1)} %get-tuple-element.14), channel_id=1, source_target_pairs={{0,6},{1,7},{2,0},{3,1},{4,2},{5,3},{6,4},{7,5},{8,14},{9,15},{10,... | collective-permute-start | bytes 98312 | tf_op jit(solution)/shard_map/ppermute | solution.py:341
  36.1 5.4 %collective-permute-start.1 = (f32[32,256]{1,0:T(8,128)S(1)}, f32[32,256]{1,0:T(8,128)S(1)}, u32[]{:S(2)}, u32[]{:S(2)}) collective-permute-start(f32[32,256]{1,0:T(8,128)S(1)} %get-tuple-element.14), channel_id=1, source_target_pairs={{0,4},{1,5},{2,6},{3,7},{4,0},{5,1},{6,2},{7,3},{8,12},{9,13},{10,... | collective-permute-start | bytes 98312 | tf_op jit(solution)/shard_map/ppermute | solution.py:341
  36.9 5.1 %collective-permute-start = (f32[32,256]{1,0:T(8,128)S(1)}, f32[32,256]{1,0:T(8,128)S(1)}, u32[]{:S(2)}, u32[]{:S(2)}) collective-permute-start(f32[32,256]{1,0:T(8,128)S(1)} %get-tuple-element.14), channel_id=1, source_target_pairs={{0,2},{1,3},{2,4},{3,5},{4,6},{5,7},{6,0},{7,1},{8,10},{9,11},{10,... | collective-permute-start | bytes 98312 | tf_op jit(solution)/shard_map/ppermute | solution.py:341
  42.1 18.2 %collective-permute-start.3 = (f32[4,32,256]{2,1,0:T(8,128)S(1)}, f32[4,32,256]{2,1,0:T(8,128)S(1)}, u32[]{:S(2)}, u32[]{:S(2)}) collective-permute-start(f32[4,32,256]{2,1,0:T(8,128)S(1)} %pad_maximum_fusion.same_ref), channel_id=1, source_target_pairs={{0,1},{1,0},{2,3},{3,2},{4,5},{5,4},{6,7},{7,6},{8,9},{9,8},{10,11... | collective-permute-start | bytes 393224 | tf_op jit(solution)/shard_map/ppermute | solution.py:343
  53.6 3.7 %collective-permute-start.6 = (f32[32,128]{1,0:T(8,128)S(1)}, f32[32,128]{1,0:T(8,128)S(1)}, u32[]{:S(2)}, u32[]{:S(2)}) collective-permute-start(f32[32,128]{1,0:T(8,128)S(1)} %bitcast.9), channel_id=1, source_target_pairs={{0,6},{1,7},{2,0},{3,1},{4,2},{5,3},{6,4},{7,5},{8,14},{9,15},{10,... | collective-permute-start | bytes 49160 | tf_op jit(solution)/shard_map/ppermute | solution.py:346
  54.0 5.2 %collective-permute-start.5 = (f32[32,128]{1,0:T(8,128)S(1)}, f32[32,128]{1,0:T(8,128)S(1)}, u32[]{:S(2)}, u32[]{:S(2)}) collective-permute-start(f32[32,128]{1,0:T(8,128)S(1)} %bitcast.10), channel_id=1, source_target_pairs={{0,4},{1,5},{2,6},{3,7},{4,0},{5,1},{6,2},{7,3},{8,12},{9,13},{10,... | collective-permute-start | bytes 49160 | tf_op jit(solution)/shard_map/ppermute | solution.py:346
  55.3 4.9 %collective-permute-start.4 = (f32[32,128]{1,0:T(8,128)S(1)}, f32[32,128]{1,0:T(8,128)S(1)}, u32[]{:S(2)}, u32[]{:S(2)}) collective-permute-start(f32[32,128]{1,0:T(8,128)S(1)} %bitcast.11), channel_id=1, source_target_pairs={{0,2},{1,3},{2,4},{3,5},{4,6},{5,7},{6,0},{7,1},{8,10},{9,11},{10,... | collective-permute-start | bytes 49160 | tf_op jit(solution)/shard_map/ppermute | solution.py:346

commit v8 on v7

--- a/solution.py
+++ b/solution.py
@@ -266,12 +266,9 @@
     share_ref[...] = jnp.broadcast_to(share, share_ref.shape)
 
 
-def scatter_body(
-    driven_ref, same_ref, other_ref, share_0, share_1, share_2, share_3, own_ref, out_ref, *, width
-):
+def pick_body(driven_ref, same_ref, other_ref, own_ref, made_ref):
     ports = own_ref.shape[0]
-    shares = (share_0, share_1, share_2, share_3)
-    chips = len(shares)
+    chips = same_ref.shape[0]
     place = lax.axis_index("port")
     driven = driven_ref[...]
     holder = driven // ports
@@ -289,6 +286,23 @@
             term = left.astype(jnp.bfloat16)
             q = q + jnp.dot(picks, term, preferred_element_type=jnp.float32)
             left = left - term.astype(jnp.float32)
+    q_re, q_im = q[:, :LANES], q[:, LANES:]
+    b_re, b_im = own_ref[:, :LANES], own_ref[:, LANES:]
+    made_ref[0] = b_re * q_re + b_im * q_im
+    made_ref[1] = b_im * q_re - b_re * q_im
+    made_ref[2] = q_re * q_re + q_im * q_im
+
+
+def scatter_body(driven_ref, share_0, share_1, share_2, share_3, made_ref, out_ref, *, width):
+    ports = out_ref.shape[1]
+    shares = (share_0, share_1, share_2, share_3)
+    chips = len(shares)
+    driven = driven_ref[...]
+    holder = driven // ports
+    rest = driven % ports
+    back = (lax.axis_index("port") // 2 - holder // 2) & (chips - 1)
+    core = holder & 1
+    lane = lax.broadcasted_iota(jnp.int32, (ports, LANES), 1)
     level = jnp.zeros((ports, LANES), jnp.float32)
     sender = lax.broadcasted_iota(jnp.int32, share_0.shape, 0) & 1
     for k in range(chips):
@@ -297,12 +311,9 @@
             summed = jnp.sum(summed, axis=0, keepdims=True)
             level = level + jnp.where((lane == rest) & (back == k) & (core == c), summed, 0.0)
     mean = jnp.sum(level, axis=1, keepdims=True) / width + 1e-06
-    q_re, q_im = q[:, :LANES], q[:, LANES:]
-    b_re, b_im = own_ref[:, :LANES], own_ref[:, LANES:]
-    power = q_re * q_re + q_im * q_im
-    inverse = 1.0 / jnp.maximum(power, 0.1 * mean)
-    out_ref[0] = (b_re * q_re + b_im * q_im) * inverse
-    out_ref[1] = (b_im * q_re - b_re * q_im) * inverse
+    inverse = 1.0 / jnp.maximum(made_ref[2], 0.1 * mean)
+    out_ref[0] = made_ref[0] * inverse
+    out_ref[1] = made_ref[1] * inverse
 
 
 def body(voltages, currents, impedance, freq_index, window_start, pairing):
@@ -344,15 +355,20 @@
     means = [shares]
     for k in range(1, chips):
         means.append(lax.ppermute(shares, "port", ahead[k - 1]))
+    made = pl.pallas_call(
+        pick_body,
+        in_specs=[VMEM] * 4,
+        out_specs=VMEM,
+        out_shape=pltpu.VMEM((3, ports, LANES), jnp.float32),
+        name="pick",
+    )(in_vmem(driven), in_vmem(same), in_vmem(other), in_vmem(own))
     return pl.pallas_call(
         functools.partial(scatter_body, width=width),
-        in_specs=[VMEM] * (chips + 4),
+        in_specs=[VMEM] * (chips + 2),
         out_specs=VMEM,
         out_shape=jax.ShapeDtypeStruct((2, ports, LANES), jnp.float32),
         name="scatter",
-    )(
-        in_vmem(driven), in_vmem(same), in_vmem(other), *map(in_vmem, means), in_vmem(own),
-    )
+    )(in_vmem(driven), *map(in_vmem, means), in_vmem(made))
 
 
 def solution(mesh):

time: 61.3 us -> 61.2 us (level)
  no operation moved by 1% of the time
where the time goes in v8:
time: 61.2 us; the launch traced here: 61 us
  blocking collectives  36.2 us (59%)
  Pallas kernels  9.47 us (15%)
  waiting for transfers between devices  7.77 us (13%)
  starting transfers between devices  7.54 us (12%)
    all_to_all x1, blocking collectives, body(): parts = lax.all_to_all(in_vmem(parts), 'tm', 0, 0, tiled=True)  24.8 us
    all_to_all x1, blocking collectives, body(): lax.all_to_all(in_vmem(share), ('tm', 'port'), 0, 0, tiled=True, axis_ind...  11.4 us
    pallas_call x1, Pallas kernels, transform(): pl.pallas_call(functools.partial(transform_body, inner=INNER, total=total...  8.3 us
    ppermute x3, starting transfers between devices, body(): along.append(lax.ppermute(sent, 'port', ahead[k - 1]))  4.51 us
    ppermute x3, waiting for transfers between devices, body(): along.append(lax.ppermute(sent, 'port', ahead[k - 1]))  4.24 us
    ppermute x3, waiting for transfers between devices, body(): means.append(lax.ppermute(shares, 'port', ahead[k - 1]))  3.53 us
    ppermute x3, starting transfers between devices, body(): means.append(lax.ppermute(shares, 'port', ahead[k - 1]))  2.94 us
  transfers between devices with their start and end apart: 7, of which 5 were waited for; matrix products, arithmetic and copies ran while one was open for 0% of the time, Pallas kernels for 0%

profile of v8, /device:TPU:0, one launch (start us, length us, event | category | flops | bytes accessed | tf_op | source)
XLA Modules:
  0.0 61.0 jit_solution(15840493894609713959)
XLA Ops:
  0.0 8.3 %spectrum.1 = (f32[16,128,128]{2,1,0:T(8,128)S(1)}, f32[32,128]{1,0:T(8,128)S(1)}, s32[32,128]{1,0:T(8,128)S(1)}) custom-call(s32[32]{0:T(128)} %start_ref.1, f32[32]{0:T(128)} %impedance_ref.1, s32[32]{0:T(128)} %pairing_ref.1, s32[1,2048]{1,0:T(1,128)} %bitcast.18, f32[32,16384]{1,0:T(8,128)} %v_ref.1, f32[32,16384]{1,0:T(8,128)} %c_ref.1), custom_call_target="tpu_custom_call" | custom-call | tf_op jit(solution)/shard_map/spectrum/pallas_call | solution.py:207
  8.3 24.8 %all_to_all.16.parts_ref = f32[16,128,128]{2,1,0:T(8,128)S(1)} all-to-all(f32[16,128,128]{2,1,0:T(8,128)S(1)} %get-tuple-element.13), channel_id=1, replica_groups=mesh['tm'=16,'port'=8] {'tm'}, dimensions={0} | all-to-all | bytes 2097152 | tf_op jit(solution)/shard_map/all_to_all | solution.py:328
  33.1 0.2 waves.1
  33.3 2.8 %collective-permute-start.5 = (f32[32,256]{1,0:T(8,128)S(1)}, f32[32,256]{1,0:T(8,128)S(1)}, u32[]{:S(2)}, u32[]{:S(2)}) collective-permute-start(f32[32,256]{1,0:T(8,128)S(1)} %get-tuple-element.15), channel_id=1, source_target_pairs={{0,6},{1,7},{2,0},{3,1},{4,2},{5,3},{6,4},{7,5},{8,14},{9,15},{10,... | collective-permute-start | bytes 98312 | tf_op jit(solution)/shard_map/ppermute | solution.py:352
  36.1 0.8 %collective-permute-start.4 = (f32[32,256]{1,0:T(8,128)S(1)}, f32[32,256]{1,0:T(8,128)S(1)}, u32[]{:S(2)}, u32[]{:S(2)}) collective-permute-start(f32[32,256]{1,0:T(8,128)S(1)} %get-tuple-element.15), channel_id=1, source_target_pairs={{0,4},{1,5},{2,6},{3,7},{4,0},{5,1},{6,2},{7,3},{8,12},{9,13},{10,... | collective-permute-start | bytes 98312 | tf_op jit(solution)/shard_map/ppermute | solution.py:352
  36.9 0.9 %collective-permute-start.3 = (f32[32,256]{1,0:T(8,128)S(1)}, f32[32,256]{1,0:T(8,128)S(1)}, u32[]{:S(2)}, u32[]{:S(2)}) collective-permute-start(f32[32,256]{1,0:T(8,128)S(1)} %get-tuple-element.15), channel_id=1, source_target_pairs={{0,2},{1,3},{2,4},{3,5},{4,6},{5,7},{6,0},{7,1},{8,10},{9,11},{10,... | collective-permute-start | bytes 98312 | tf_op jit(solution)/shard_map/ppermute | solution.py:352
  37.8 0.0 collective-permute-done.5
  37.8 3.7 %collective-permute-done.4 = f32[32,256]{1,0:T(8,128)S(1)} collective-permute-done((f32[32,256]{1,0:T(8,128)S(1)}, f32[32,256]{1,0:T(8,128)S(1)}, u32[]{:S(2)}, u32[]{:S(2)}) %collective-permute-start.4) | collective-permute-done | bytes 32800 | tf_op jit(solution)/shard_map/ppermute | solution.py:352
  41.5 0.5 collective-permute-done.3
  42.1 0.1 collective-permute-start.6
  42.2 11.4 %all_to_all.17 = f32[32,1,128]{2,1,0:T(1,128)S(1)} all-to-all(f32[32,1,128]{2,1,0:T(1,128)S(1)} %bitcast.14), channel_id=1, replica_groups={{0,1,8,9,16,17,24,25,32,33,40,41,48,49,56,57,64,65,72,73,80,81,88,89,96..., dimensions={0} | all-to-all | bytes 32768 | tf_op jit(solution)/shard_map/all_to_all | solution.py:347
  53.6 0.4 collective-permute-start.2
  54.0 1.3 %collective-permute-start.1 = (f32[32,128]{1,0:T(8,128)S(1)}, f32[32,128]{1,0:T(8,128)S(1)}, u32[]{:S(2)}, u32[]{:S(2)}) collective-permute-start(f32[32,128]{1,0:T(8,128)S(1)} %bitcast.10), channel_id=1, source_target_pairs={{0,4},{1,5},{2,6},{3,7},{4,0},{5,1},{6,2},{7,3},{8,12},{9,13},{10,... | collective-permute-start | bytes 49160 | tf_op jit(solution)/shard_map/ppermute | solution.py:357
  55.3 1.2 %collective-permute-start = (f32[32,128]{1,0:T(8,128)S(1)}, f32[32,128]{1,0:T(8,128)S(1)}, u32[]{:S(2)}, u32[]{:S(2)}) collective-permute-start(f32[32,128]{1,0:T(8,128)S(1)} %bitcast.11), channel_id=1, source_target_pairs={{0,2},{1,3},{2,4},{3,5},{4,6},{5,7},{6,0},{7,1},{8,10},{9,11},{10,... | collective-permute-start | bytes 49160 | tf_op jit(solution)/shard_map/ppermute | solution.py:357
  56.5 0.0 collective-permute-done.6.other_ref
  56.5 0.2 pick.1.made_ref
  56.7 0.6 collective-permute-done.2.share_3
  57.3 1.9 %collective-permute-done.1.share_2 = f32[32,128]{1,0:T(8,128)S(1)} collective-permute-done((f32[32,128]{1,0:T(8,128)S(1)}, f32[32,128]{1,0:T(8,128)S(1)}, u32[]{:S(2)}, u32[]{:S(2)}) %collective-permute-start.1) | collective-permute-done | bytes 16416 | tf_op jit(solution)/shard_map/ppermute | solution.py:357
  59.2 1.0 %collective-permute-done.share_1 = f32[32,128]{1,0:T(8,128)S(1)} collective-permute-done((f32[32,128]{1,0:T(8,128)S(1)}, f32[32,128]{1,0:T(8,128)S(1)}, u32[]{:S(2)}, u32[]{:S(2)}) %collective-permute-start) | collective-permute-done | bytes 16416 | tf_op jit(solution)/shard_map/ppermute | solution.py:357
  60.3 0.8 %scatter.1 = f32[2,32,128]{2,1,0:T(8,128)} custom-call(s32[32,128]{1,0:T(8,128)S(1)} %get-tuple-element.11.driven_ref, f32[32,128]{1,0:T(8,128)S(1)} %bitcast.12, f32[32,128]{1,0:T(8,128)S(1)} %collective-permute-done.share_1, f32[32,128]{1,0:T(8,128)S(1)} %collective-permute-done.1.share_2, f32[32,128]{1,0:T(8,128)S(1)} %collective-permute-done.2.share_3, ...), custom_call_target="tpu_custom_call" | custom-call | tf_op jit(solution)/shard_map/scatter/pallas_call | solution.py:365
  (1 shorter events, 0.0 us)
Async XLA Ops:
  33.3 4.5 %collective-permute-start.5 = (f32[32,256]{1,0:T(8,128)S(1)}, f32[32,256]{1,0:T(8,128)S(1)}, u32[]{:S(2)}, u32[]{:S(2)}) collective-permute-start(f32[32,256]{1,0:T(8,128)S(1)} %get-tuple-element.15), channel_id=1, source_target_pairs={{0,6},{1,7},{2,0},{3,1},{4,2},{5,3},{6,4},{7,5},{8,14},{9,15},{10,... | collective-permute-start | bytes 98312 | tf_op jit(solution)/shard_map/ppermute | solution.py:352
  36.1 5.4 %collective-permute-start.4 = (f32[32,256]{1,0:T(8,128)S(1)}, f32[32,256]{1,0:T(8,128)S(1)}, u32[]{:S(2)}, u32[]{:S(2)}) collective-permute-start(f32[32,256]{1,0:T(8,128)S(1)} %get-tuple-element.15), channel_id=1, source_target_pairs={{0,4},{1,5},{2,6},{3,7},{4,0},{5,1},{6,2},{7,3},{8,12},{9,13},{10,... | collective-permute-start | bytes 98312 | tf_op jit(solution)/shard_map/ppermute | solution.py:352
  36.9 5.1 %collective-permute-start.3 = (f32[32,256]{1,0:T(8,128)S(1)}, f32[32,256]{1,0:T(8,128)S(1)}, u32[]{:S(2)}, u32[]{:S(2)}) collective-permute-start(f32[32,256]{1,0:T(8,128)S(1)} %get-tuple-element.15), channel_id=1, source_target_pairs={{0,2},{1,3},{2,4},{3,5},{4,6},{5,7},{6,0},{7,1},{8,10},{9,11},{10,... | collective-permute-start | bytes 98312 | tf_op jit(solution)/shard_map/ppermute | solution.py:352
  42.1 14.4 %collective-permute-start.6 = (f32[4,32,256]{2,1,0:T(8,128)S(1)}, f32[4,32,256]{2,1,0:T(8,128)S(1)}, u32[]{:S(2)}, u32[]{:S(2)}) collective-permute-start(f32[4,32,256]{2,1,0:T(8,128)S(1)} %pad_maximum_fusion.same_ref), channel_id=1, source_target_pairs={{0,1},{1,0},{2,3},{3,2},{4,5},{5,4},{6,7},{7,6},{8,9},{9,8},{10,11... | collective-permute-start | bytes 393224 | tf_op jit(solution)/shard_map/ppermute | solution.py:354
  53.6 3.7 %collective-permute-start.2 = (f32[32,128]{1,0:T(8,128)S(1)}, f32[32,128]{1,0:T(8,128)S(1)}, u32[]{:S(2)}, u32[]{:S(2)}) collective-permute-start(f32[32,128]{1,0:T(8,128)S(1)} %bitcast.9), channel_id=1, source_target_pairs={{0,6},{1,7},{2,0},{3,1},{4,2},{5,3},{6,4},{7,5},{8,14},{9,15},{10,... | collective-permute-start | bytes 49160 | tf_op jit(solution)/shard_map/ppermute | solution.py:357
  54.0 5.2 %collective-permute-start.1 = (f32[32,128]{1,0:T(8,128)S(1)}, f32[32,128]{1,0:T(8,128)S(1)}, u32[]{:S(2)}, u32[]{:S(2)}) collective-permute-start(f32[32,128]{1,0:T(8,128)S(1)} %bitcast.10), channel_id=1, source_target_pairs={{0,4},{1,5},{2,6},{3,7},{4,0},{5,1},{6,2},{7,3},{8,12},{9,13},{10,... | collective-permute-start | bytes 49160 | tf_op jit(solution)/shard_map/ppermute | solution.py:357
  55.3 4.9 %collective-permute-start = (f32[32,128]{1,0:T(8,128)S(1)}, f32[32,128]{1,0:T(8,128)S(1)}, u32[]{:S(2)}, u32[]{:S(2)}) collective-permute-start(f32[32,128]{1,0:T(8,128)S(1)} %bitcast.11), channel_id=1, source_target_pairs={{0,2},{1,3},{2,4},{3,5},{4,6},{5,7},{6,0},{7,1},{8,10},{9,11},{10,... | collective-permute-start | bytes 49160 | tf_op jit(solution)/shard_map/ppermute | solution.py:357
